TPU v7x, 256 devices: a whole 4x4x8 slice. The times are simulated.
256 devices in a mesh: layer: 4 (over z_lo, core), harm: 64 (over y, z_hi, x).
Axes of the slice: x: 4, y: 4, z: 8 (z_hi: 4, z_lo: 2; z = z_hi * 2 + z_lo), core: 2. Of those that a mesh axis runs over, the one named last changes fastest.
Arguments:
- source: bfloat16 [2, 2048, 128], P(None, 'harm'), may hold values from -6 to 6
- transfer: bfloat16 [4, 2, 2048, 2048], P('layer', None, 'harm'), may hold values from -0.09375 to 0.09375
- fields: bfloat16 [4, 2, 2048, 128], P('layer', None, 'harm'), may hold values from -6 to 6
- orders: int32 [2048], replicated, may hold values from 0 to 2047, each once
Outputs:
- gradients: float32 [4, 2, 4096], P('layer', None, 'harm')
- boundary: bfloat16 [4, 2, 2048, 128], P('layer', None, 'harm')
Inputs may be any that keep to these rules, and one draw needn't show every extreme that they name: `orders`: every value from 0 to 2047 appears exactly once.
All inputs are finite; a program needn't handle non-finite values.
Results may differ from a plain program's by a relative error of at most 0.006.
Values may be sent and summed in bfloat16 or wider, within the bound.
A program may use at most 64 MiB of HBM per device.

v0:
```python
import math

import jax
import jax.numpy as jnp
from jax import lax
from jax.sharding import PartitionSpec as P


def in_order(blocks, dim):
    blocks = jnp.moveaxis(blocks, 0, dim)
    dims = blocks.shape
    return blocks.reshape(*dims[:dim], dims[dim] * dims[dim + 1], *dims[dim + 2 :])


def from_everyone(value, axis):
    copies = jnp.broadcast_to(value, (lax.axis_size(axis), *value.shape))
    return lax.all_to_all(copies, axis, split_axis=0, concat_axis=0, tiled=True)


def gather_directly(value, axis, dim):
    return in_order(from_everyone(value, axis), dim)


def shifted(value, axis, steps):
    count = lax.axis_size(axis)
    first, last = (max(0, -steps), min(count, count - steps))
    return lax.ppermute(value, axis, [(source, source + steps) for source in range(first, last)])


def correlate(adjoint, forward, position, band_start, band_width):
    harmonics = adjoint.shape[1]
    columns = adjoint.shape[2]
    adj_sorted = jnp.take(adjoint, position, axis=1)
    fwd_sorted = jnp.take(forward, position, axis=1)
    padded = jnp.pad(adj_sorted, ((0, 0), (harmonics, harmonics + 1), (0, 0)))
    window_slab = lax.dynamic_slice_in_dim(padded, band_start + 1, harmonics + band_width, 1)
    count = harmonics // band_width
    blocks = window_slab.reshape(2, count + 1, band_width, columns)
    windows = jnp.concatenate([blocks[:, :-1], blocks[:, 1:]], axis=2)
    forward_blocks = fwd_sorted.reshape(2, count, band_width, columns)

    def product(left_part, right_part):
        return jnp.einsum("nkb,ncb->nkc", left_part, right_part, preferred_element_type=jnp.float32)

    real_part = product(forward_blocks[0], windows[0]) - product(forward_blocks[1], windows[1])
    imag_part = product(forward_blocks[0], windows[1]) + product(forward_blocks[1], windows[0])

    def diagonals(result_block):
        flattened = result_block.reshape(count, band_width * 2 * band_width)
        flattened = jnp.pad(flattened, ((0, 0), (0, band_width)))
        shaped = flattened.reshape(count, band_width, 2 * band_width + 1)[:, :, :band_width]
        return jnp.sum(shaped, axis=(0, 1))

    return jnp.stack([diagonals(real_part), diagonals(imag_part)])


def gather_rows(adjoint):
    return lax.all_gather(adjoint, "harm", axis=1, tiled=True)


def spread_fields(local_fields):
    return gather_directly(local_fields, "harm", 2)


def propagate(matrix, gathered):
    real_part = jnp.dot(matrix[0], gathered[0], preferred_element_type=jnp.float32) - jnp.dot(
        matrix[1], gathered[1], preferred_element_type=jnp.float32
    )
    imag_part = jnp.dot(matrix[0], gathered[1], preferred_element_type=jnp.float32) + jnp.dot(
        matrix[1], gathered[0], preferred_element_type=jnp.float32
    )
    return jnp.stack([real_part, imag_part]).astype(jnp.bfloat16)


def per_device(source, transfer, fields, orders):
    harmonics = orders.shape[0]
    sections = lax.axis_size("layer")
    section_index = lax.axis_index("layer")
    band_width = 2 * harmonics // lax.axis_size("harm")
    band_start = lax.axis_index("harm") * band_width
    rows_dev = transfer.shape[2]
    columns = source.shape[2]
    norm_scale = 1.0 / math.sqrt(harmonics * columns)
    position = (
        jnp.zeros((harmonics,), jnp.int32).at[orders].set(jnp.arange(harmonics, dtype=jnp.int32))
    )
    layers_here = transfer.shape[0]
    field_source = spread_fields(fields)
    micro_count = 1
    micro_cols = columns // micro_count
    stored = jnp.zeros((layers_here, 2, harmonics, columns), jnp.bfloat16)
    bottom = jnp.zeros((2, rows_dev, columns), jnp.bfloat16)
    incoming = jnp.zeros((2, rows_dev, micro_cols), jnp.bfloat16)
    total_steps = sections + micro_count - 1
    for step_index in range(total_steps):
        micro_index = step_index - (sections - 1 - section_index)
        active = (micro_index >= 0) & (micro_index < micro_count)
        if step_index < micro_count:
            top_source = source
        else:
            top_source = jnp.zeros_like(incoming)
        adjoint = jnp.where(section_index == sections - 1, top_source, incoming)
        gathered = gather_rows(adjoint)
        stored = stored.at[0].set(jnp.where(active, gathered, stored[0]))
        adjoint = propagate(transfer[0], gathered)
        bottom = jnp.where(active, adjoint, bottom)
        if step_index < total_steps - 1:
            incoming = shifted(adjoint, "layer", -1)
    grads = jnp.stack(
        [correlate(stored[0], field_source[0], position, band_start, band_width) * norm_scale]
    )
    return (grads, bottom[None])


def solution(mesh):
    return jax.shard_map(
        per_device,
        mesh=mesh,
        in_specs=(
            P(None, "harm", None),
            P("layer", None, "harm", None),
            P("layer", None, "harm", None),
            P(),
        ),
        out_specs=(P("layer", None, "harm"), P("layer", None, "harm", None)),
        check_vma=False,
    )
```

profile of v0, /device:TPU:2, one launch (start us, length us, event | category | flops | bytes accessed | tf_op | source)
XLA Modules:
  0.0 404.4 jit_solution(10969838108467156854)
XLA Ops:
  7.2 0.6 broadcast_select_fusion.5
  8.0 81.2 %all-gather.5.cloned.1.call-done = bf16[2,2048,128]{2,1,0:T(8,128)(2,1)} async-done(((bf16[2,32,128]{2,1,0:T(8,128)(2,1)}), bf16[2,2048,128]{2,1,0:T(8,128)(2,1)}) %all-gather.5.cloned.1.call-update) | async-done | bytes 1048592 | tf_op jit(solution)/shard_map/all_gather | solution.py:58
  89.2 1.4 fusion.15
  90.6 1.3 fusion.16
  91.9 1.3 fusion
  93.5 1.3 collective-permute-start
  94.8 1.8 collective-permute-done
  96.6 0.6 broadcast_select_fusion.4
  97.3 72.2 %all-gather.7.cloned.1.call-done = bf16[2,2048,128]{2,1,0:T(8,128)(2,1)} async-done(((bf16[2,32,128]{2,1,0:T(8,128)(2,1)}), bf16[2,2048,128]{2,1,0:T(8,128)(2,1)}) %all-gather.7.cloned.1.call-update) | async-done | bytes 1048592 | tf_op jit(solution)/shard_map/all_gather | solution.py:58
  169.5 1.3 fusion.18
  170.8 1.2 fusion.17
  172.1 1.3 fusion.2
  173.6 1.3 collective-permute-start.1
  174.9 1.8 collective-permute-done.1
  176.7 0.6 broadcast_select_fusion.3
  177.3 72.3 %all-gather.9.cloned.1.call-done = bf16[2,2048,128]{2,1,0:T(8,128)(2,1)} async-done(((bf16[2,32,128]{2,1,0:T(8,128)(2,1)}), bf16[2,2048,128]{2,1,0:T(8,128)(2,1)}) %all-gather.9.cloned.1.call-update) | async-done | bytes 1048592 | tf_op jit(solution)/shard_map/all_gather | solution.py:58
  249.6 1.3 fusion.20
  250.9 1.2 fusion.19
  252.2 1.3 fusion.4
  253.7 1.3 collective-permute-start.2
  255.0 1.2 broadcast_in_dim.17
  256.2 8.8 %all-to-all-start = ((bf16[64,1,2,32,128]{4,3,2,1,0:T(8,128)(2,1)}), bf16[64,1,2,32,128]{4,3,2,1,0:T(8,128)(2,1)S(1)}, u32[]{:S(2)}, u32[]{:S(2)}) async-start(bf16[64,1,2,32,128]{4,3,2,1,0:T(8,128)(2,1)} %broadcast_in_dim.17), calls=%async_computation | async-start | bytes 2097152 | tf_op jit(solution)/shard_map/all_to_all | solution.py:17
  265.1 0.6 broadcast_select_fusion.2
  265.8 8.2 %scatter_custom_fusion = s32[2048]{0:T(1024)S(1)} fusion(s32[2048]{0:T(1024)S(1)} %compare_select_fusion.1, s32[2048]{0:T(1024)S(1)} %iota.3, s32[]{:T(128)} %constant.110.clone.1), kind=kCustom, calls=%fused_computation.103 | custom fusion | bytes 8196 | tf_op jit(solution)/shard_map/scatter | solution.py:85
  274.0 22.8 %all-to-all-done = bf16[64,1,2,32,128]{4,3,2,1,0:T(8,128)(2,1)S(1)} async-done(((bf16[64,1,2,32,128]{4,3,2,1,0:T(8,128)(2,1)}), bf16[64,1,2,32,128]{4,3,2,1,0:T(8,128)(2,1)S(1)}, u32[]{:S(2)}, u32[]{:S(2)}) %all-to-all-start) | async-done | bytes 1048608 | tf_op jit(solution)/shard_map/all_to_all | solution.py:17
  296.9 8.7 %copy.13 = bf16[2,2048,128]{2,0,1:T(2,128)(2,1)S(1)} copy(bf16[2,2048,128]{2,1,0:T(8,128)(2,1)S(1)} %bitcast.145) | data formatting | bytes 2097152 | tf_op jit(solution)/shard_map/squeeze;reshape | solution.py:110
  305.6 7.1 %gather_fusion = bf16[2048,2,128]{2,1,0:T(2,128)(2,1)S(1)} fusion(bf16[2,2048,128]{2,0,1:T(2,128)(2,1)S(1)} %copy.13, s32[2048]{0:T(1024)S(1)} %fusion.58), kind=kCustom, calls=%fused_computation.clone | custom fusion | bytes 2105344 | tf_op jit(solution)/shard_map/jit(_take)/gather | solution.py:34
  312.7 34.6 %all-gather.11.cloned.1.call-done = bf16[2,2048,128]{2,1,0:T(8,128)(2,1)} async-done(((bf16[2,32,128]{2,1,0:T(8,128)(2,1)}), bf16[2,2048,128]{2,1,0:T(8,128)(2,1)}) %all-gather.11.cloned.1.call-update) | async-done | bytes 1048592 | tf_op jit(solution)/shard_map/all_gather | solution.py:58
  347.3 1.4 select_select_fusion
  348.8 8.7 %copy.14 = bf16[2,2048,128]{2,0,1:T(2,128)(2,1)S(1)} copy(bf16[2,2048,128]{2,1,0:T(8,128)(2,1)S(1)} %select_select_fusion) | data formatting | bytes 2097152 | tf_op jit(solution)/shard_map/jit(_where)/select_n | solution.py:104
  357.4 7.1 %gather_fusion.1 = bf16[2048,2,128]{2,1,0:T(2,128)(2,1)S(1)} fusion(bf16[2,2048,128]{2,0,1:T(2,128)(2,1)S(1)} %copy.14, s32[2048]{0:T(1024)S(1)} %fusion.58), kind=kCustom, calls=%fused_computation.1.clone | custom fusion | bytes 2105344 | tf_op jit(solution)/shard_map/jit(_take)/gather | solution.py:33
  364.5 7.6 %fusion.14 = (bf16[2,2048,128]{2,0,1:T(2,128)(2,1)S(1)}, bf16[2,2048,128]{2,0,1:T(2,128)(2,1)S(1)}) fusion(bf16[2048,2,128]{2,1,0:T(2,128)(2,1)S(1)} %gather_fusion.1, pred[2048]{0:T(1024)(128)(4,1)S(1)} %compare_and_fusion, bf16[2048,2,128]{2,1,0:T(2,128)(2,1)S(1)} %gather_fusion), kind=kLoop, calls=%fused_computation.38 | loop fusion | flops 1048576 | bytes 4196352 | tf_op jit(solution)/shard_map/jit(_take)/select_n | solution.py:33
  372.1 6.4 %pad_dynamic-slice_fusion = bf16[2,2112,128]{2,0,1:T(2,128)(2,1)S(1)} fusion(s32[]{:T(128)S(6)} %select_n.125, bf16[2,2048,128]{2,0,1:T(2,128)(2,1)S(1)} %get-tuple-element.55), kind=kLoop, calls=%fused_computation.3 | loop fusion | bytes 2129924 | tf_op jit(solution)/shard_map/dynamic_slice | solution.py:36
  378.7 0.6 fusion.66
  379.3 1.5 fusion.67
  380.9 0.8 fusion.23
  381.7 0.8 fusion.64
  382.6 0.8 convolution_add_fusion
  383.4 0.6 copy.22
  384.1 0.8 convolution_subtract_fusion
  384.9 0.6 copy.23
  385.6 1.1 pad.20
  386.6 3.8 reshape.351
  390.7 2.7 reshape.353
  393.7 0.6 maximum_multiply_fusion
  394.3 1.2 fusion.22
  395.5 1.2 fusion.21
  397.2 0.6 maximum_select_fusion
  (42 shorter events, 2.3 us)
Async XLA Ops:
  7.2 86.1 %copy-start.6 = (bf16[1,2,32,2048]{3,2,1,0:T(8,128)(2,1)S(1)}, bf16[1,2,32,2048]{3,2,1,0:T(8,128)(2,1)}, u32[]{:S(2)}) copy-start(bf16[1,2,32,2048]{3,2,1,0:T(8,128)(2,1)} %param.15) | copy-start | bytes 786436
  7.2 82.0 %all-gather.5.cloned.1.call-start = ((), (), s32[]{:S(2)}) async-start(), calls=%async_computation.1 | async-start | bytes 1064960 | tf_op jit(solution)/shard_map/all_gather | solution.py:58
  7.9 161.6 %all-gather.7.cloned.1.call-start = ((), (), s32[]{:S(2)}) async-start(), calls=%async_computation.2 | async-start | bytes 1064960 | tf_op jit(solution)/shard_map/all_gather | solution.py:58
  89.2 4.1 %copy-start = (bf16[2,2048,128]{2,1,0:T(8,128)(2,1)S(1)}, bf16[2,2048,128]{2,1,0:T(8,128)(2,1)}, u32[]{:S(2)}) copy-start(bf16[2,2048,128]{2,1,0:T(8,128)(2,1)} %all-gather.5.cloned.1.call-done) | copy-start | bytes 3145732
  93.5 3.1 collective-permute-start
  97.2 152.4 %all-gather.9.cloned.1.call-start = ((), (), s32[]{:S(2)}) async-start(), calls=%async_computation.3 | async-start | bytes 1064960 | tf_op jit(solution)/shard_map/all_gather | solution.py:58
  169.5 3.9 copy-start.1
  172.1 82.9 %copy-start.4 = (bf16[1,2,32,128]{3,2,1,0:T(8,128)(2,1)S(1)}, bf16[1,2,32,128]{3,2,1,0:T(8,128)(2,1)}, u32[]{:S(2)}) copy-start(bf16[1,2,32,128]{3,2,1,0:T(8,128)(2,1)} %param.16) | copy-start | bytes 49156
  173.6 3.1 collective-permute-start.1
  249.6 3.8 copy-start.3
  253.4 12.3 %copy-start.5 = (s32[2048]{0:T(1024)S(1)}, s32[2048]{0:T(1024)}, u32[]{:S(2)}) copy-start(s32[2048]{0:T(1024)} %param.17) | copy-start | bytes 24580
  253.7 11.4 %collective-permute-start.2 = (bf16[2,32,128]{2,1,0:T(8,128)(2,1)S(1)}, bf16[2,32,128]{2,1,0:T(8,128)(2,1)S(1)}, u32[]{:S(2)}, u32[]{:S(2)}) collective-permute-start(bf16[2,32,128]{2,1,0:T(8,128)(2,1)S(1)} %pad_maximum_fusion.3), channel_id=1, source_target_pairs={{64,0},{128,64},{192,128},{65,1},{129,65},{193,129},{66,2},{130,66... | collective-permute-start | bytes 49160 | tf_op jit(solution)/shard_map/ppermute | solution.py:27
  256.2 40.6 %all-to-all-start = ((bf16[64,1,2,32,128]{4,3,2,1,0:T(8,128)(2,1)}), bf16[64,1,2,32,128]{4,3,2,1,0:T(8,128)(2,1)S(1)}, u32[]{:S(2)}, u32[]{:S(2)}) async-start(bf16[64,1,2,32,128]{4,3,2,1,0:T(8,128)(2,1)} %broadcast_in_dim.17), calls=%async_computation | async-start | bytes 2097152 | tf_op jit(solution)/shard_map/all_to_all | solution.py:17
  265.0 82.3 %all-gather.11.cloned.1.call-start = ((), (), s32[]{:S(2)}) async-start(), calls=%async_computation.4 | async-start | bytes 1064960 | tf_op jit(solution)/shard_map/all_gather | solution.py:58
  393.4 3.4 copy-start.2
Sparse Core Ops, SparseCore 0:
  11.7 77.4 all-gather.4
  97.3 72.1 all-gather.6
  177.4 72.1 all-gather.8
  269.2 78.0 all-gather.10
where the time goes:
time: 405 us; the launch traced here: 404 us
  waiting for transfers between devices  287 us (71%)
  local copies, waits for them, and re-layouts  58.7 us (14%)
  matrix products  18.4 us (5%)
  between operations  14.2 us (4%)
  other arithmetic  13.3 us (3%)
  starting transfers between devices  12.8 us (3%)
    all_gather x4, waiting for transfers between devices, gather_rows(): return lax.all_gather(adjoint, 'harm', axis=1, tiled=True)  260 us
    all_to_all x1, waiting for transfers between devices, from_everyone(): return lax.all_to_all(copies, axis, split_axis=0, concat_axis=0, tiled=True)  22.8 us
    all_to_all x1, starting transfers between devices, from_everyone(): return lax.all_to_all(copies, axis, split_axis=0, concat_axis=0, tiled=True)  8.8 us
    another operation x1, local copies, waits for them, and re-layouts, per_device(): field_source[0]  8.68 us
    select_n x1, local copies, waits for them, and re-layouts, per_device(): stored = stored.at[0].set(jnp.where(active, gathered, stored[0]))  8.68 us
    scatter x1, local copies, waits for them, and re-layouts, per_device(): jnp.zeros((harmonics,), jnp.int32).at[orders]  8.23 us
  transfers between devices with their start and end apart: 8, of which 7 were waited for; matrix products, arithmetic and copies ran while one was open for 6% of the time, Pallas kernels for 0%

commit v1 on v0

v1 whole, which is shorter than its diff:
```python
import functools
import math

import jax
import jax.numpy as jnp
from jax import lax
from jax.experimental import pallas as pl
from jax.experimental.pallas import tpu as pltpu
from jax.sharding import PartitionSpec as P

MESH = pl.DeviceIdType.MESH
F32 = jnp.float32
BF16 = jnp.bfloat16


def pick(total, want):
    return want if total % want == 0 else total


def kernel(
    layers, peers, scale,
    source_ref, transfer_ref, fields_ref, orders_ref, grads_ref, bound_ref,
    adj, fwd, onehot, lined, factor, outgoing,
    src_sem, out_sem, fld_sem, adj_sem, fwd_sem,
):
    group = lax.axis_index("layer")
    me = lax.axis_index("harm")
    rows = source_ref.shape[1]
    cols = source_ref.shape[2]
    harm = rows * peers
    band = 2 * rows
    blocks = harm // band
    depth = min(256, harm)
    steps = harm // depth
    others = peers - 1
    mine = pl.ds(pl.multiple_of(me * rows, rows), rows)

    def send(src, dst, send_sem, recv_sem, target, index):
        return pltpu.make_async_remote_copy(
            src_ref=src, dst_ref=dst.at[:, mine, :], send_sem=send_sem, recv_sem=recv_sem,
            device_id=(target, index), device_id_type=MESH,
        )

    def to_others(src, dst, send_sem, recv_sem, target):
        @pl.loop(1, peers)
        def _(j):
            send(src, dst, send_sem, recv_sem, target, lax.rem(me + j, peers)).start()

    def wait_bytes(buffer, sem, count):
        part = buffer.at[:, pl.ds(0, count * rows), :]
        pltpu.make_async_copy(part, part, sem).wait()

    def columns(buffer, start, size):
        at = pl.ds(start, size)
        return jnp.concatenate([buffer[0, at, :], buffer[1, at, :]], axis=1)

    def propagate():
        total = jnp.zeros((2 * rows, 2 * cols), F32)
        for k in range(steps):
            at = pl.ds(k * depth, depth)
            matrix = jnp.concatenate([transfer_ref[0, 0, :, at], transfer_ref[0, 1, :, at]], axis=0)
            total += jnp.dot(matrix, columns(adj, k * depth, depth), preferred_element_type=F32)
        real = total[:rows, :cols] - total[rows:, cols:]
        imag = total[:rows, cols:] + total[rows:, :cols]
        result = jnp.stack([real, imag]).astype(BF16)
        bound_ref[0] = result
        outgoing[...] = result

        @pl.when(group > 0)
        def _():
            below = jnp.maximum(group - 1, 0)

            @pl.loop(0, peers)
            def _(j):
                send(outgoing, adj, out_sem, adj_sem, below, lax.rem(me + j, peers)).start()

    @pl.when(group == layers - 1)
    def _():
        to_others(source_ref, adj, src_sem, adj_sem, layers - 1)
        adj[:, mine, :] = source_ref[...]

    to_others(fields_ref.at[0], fwd, fld_sem, fwd_sem, group)
    fwd[:, mine, :] = fields_ref[0]

    border = harm - 16
    lined[pl.ds(0, border), :] = jnp.zeros((border, 2 * cols), BF16)
    lined[pl.ds(2 * harm, harm), :] = jnp.zeros((harm, 2 * cols), BF16)

    @pl.when(group == layers - 1)
    def _():
        wait_bytes(adj, adj_sem, others)
        propagate()

    chunk = min(256, harm)

    @pl.loop(0, harm // chunk)
    def _(r):
        index = lax.broadcasted_iota(jnp.int32, (chunk, depth), 0)
        order = r * chunk + (index // band) * band + (band - 1) - index % band
        for k in range(steps):
            hit = orders_ref[:, pl.ds(k * depth, depth)] == order
            onehot[pl.ds(pl.multiple_of(r * chunk, chunk), chunk), pl.ds(k * depth, depth)] = (
                jnp.where(hit, 1.0, 0.0).astype(BF16)
            )

    wait_bytes(fwd, fwd_sem, others)

    @pl.loop(0, harm // chunk)
    def _(r):
        at = pl.ds(pl.multiple_of(r * chunk, chunk), chunk)
        total = jnp.zeros((chunk, 2 * cols), F32)
        for k in range(steps):
            total += jnp.dot(
                onehot[at, pl.ds(k * depth, depth)], columns(fwd, k * depth, depth),
                preferred_element_type=F32,
            )
        for n in range(chunk // band):
            real = total[n * band : (n + 1) * band, :cols]
            imag = total[n * band : (n + 1) * band, cols:]
            pair = jnp.concatenate(
                [jnp.concatenate([real, -imag], axis=1), jnp.concatenate([imag, real], axis=1)], axis=0
            )
            factor[r * (chunk // band) + n] = pair.T.astype(BF16)

    tall = harm + 16
    part = pick(tall, 688)

    @pl.loop(0, tall // part)
    def _(r):
        order = r * part - 15 + lax.broadcasted_iota(jnp.int32, (part, depth), 0)

        @pl.loop(0, steps)
        def _(k):
            at = pl.ds(pl.multiple_of(k * depth, depth), depth)
            onehot[pl.ds(pl.multiple_of(r * part, 16), part), at] = (
                jnp.where(orders_ref[:, at] == order, 1.0, 0.0).astype(BF16)
            )

    @pl.when(group < layers - 1)
    def _():
        wait_bytes(adj, adj_sem, peers)
        propagate()

    @pl.loop(0, tall // part)
    def _(r):
        at = pl.ds(pl.multiple_of(r * part, 16), part)
        total = jnp.zeros((part, 2 * cols), F32)
        for k in range(steps):
            total += jnp.dot(
                onehot[at, pl.ds(k * depth, depth)], columns(adj, k * depth, depth),
                preferred_element_type=F32,
            )
        lined[pl.ds(pl.multiple_of(border + r * part, 16), part), :] = total.astype(BF16)

    gram = jnp.zeros((2 * band, 2 * band), F32)
    for n in range(blocks):
        window = lined[pl.ds(pl.multiple_of((me + n) * band, band), 2 * band), :]
        gram += jnp.dot(window, factor[n], preferred_element_type=F32)
    turned = pltpu.roll(gram.T, band + 1, 1, stride=1, stride_axis=0)
    real = jnp.sum(turned[:band], axis=0, keepdims=True)
    imag = jnp.sum(turned[band:], axis=0, keepdims=True)
    grads_ref[0, 0:1, :] = real[:, :band] * scale
    grads_ref[0, 1:2, :] = imag[:, band:] * scale

    wait_bytes(fwd, fld_sem, others)

    @pl.when(group == layers - 1)
    def _():
        wait_bytes(adj, src_sem, others)

    @pl.when(group > 0)
    def _():
        wait_bytes(adj, out_sem, peers)


def solution(mesh):
    layers, peers = mesh.shape["layer"], mesh.shape["harm"]

    def per_device(source, transfer, fields, orders):
        rows, cols = source.shape[1], source.shape[2]
        harm = rows * peers
        band = 2 * rows
        vmem = pl.BlockSpec(memory_space=pltpu.VMEM)
        return pl.pallas_call(
            functools.partial(kernel, layers, peers, 1.0 / math.sqrt(harm * cols)),
            out_shape=(
                jax.ShapeDtypeStruct((1, 2, band), F32),
                jax.ShapeDtypeStruct((1, 2, rows, cols), BF16),
            ),
            in_specs=[vmem] * 4,
            out_specs=(vmem, vmem),
            scratch_shapes=[
                pltpu.VMEM((2, harm, cols), BF16),
                pltpu.VMEM((2, harm, cols), BF16),
                pltpu.VMEM((harm + 16, harm), BF16),
                pltpu.VMEM((3 * harm, 2 * cols), BF16),
                pltpu.VMEM((harm // band, 2 * cols, 2 * band), BF16),
                pltpu.VMEM((2, rows, cols), BF16),
                pltpu.SemaphoreType.DMA,
                pltpu.SemaphoreType.DMA,
                pltpu.SemaphoreType.DMA,
                pltpu.SemaphoreType.DMA,
                pltpu.SemaphoreType.DMA,
            ],
            compiler_params=pltpu.CompilerParams(
                has_side_effects=True, vmem_limit_bytes=48 * 1024 * 1024
            ),
        )(source, transfer, fields, orders.reshape(1, harm))

    return jax.shard_map(
        per_device,
        mesh=mesh,
        in_specs=(
            P(None, "harm", None),
            P("layer", None, "harm", None),
            P("layer", None, "harm", None),
            P(),
        ),
        out_specs=(P("layer", None, "harm"), P("layer", None, "harm", None)),
        check_vma=False,
    )
```

time: 405 us -> 95.2 us (0.24)
  waiting for transfers between devices: 287 us -> 0 us
  Pallas kernels: 0 us -> 88.7 us
  local copies, waits for them, and re-layouts: 58.7 us -> 4.24 us
  matrix products: 18.4 us -> 0 us
  between operations: 14.2 us -> 0.65 us
  other arithmetic: 13.3 us -> 0 us
  starting transfers between devices: 12.8 us -> 0 us
    all_gather x4 -> x0, waiting for transfers between devices: 260 us -> none  [gather_rows(): return lax.all_gather(adjoint, 'harm', axis=1, tiled=True)]
    pallas_call x0 -> x1, Pallas kernels: none -> 88.7 us  [per_device(): pl.pallas_call(functools.partial(kernel, layers, peers, 1.0 / math.sqrt(h...]
    all_to_all x1 -> x0, waiting for transfers between devices: 22.8 us -> none  [from_everyone(): return lax.all_to_all(copies, axis, split_axis=0, concat_axis=0, tiled=True)]
    dot_general x20 -> x0, matrix products: 18.4 us -> none  [the longest x4 5.2 us: propagate(): jnp.dot(matrix[1], gathered[1], preferred_element_type=jnp.float32)]
    gather x2 -> x0, local copies, waits for them, and re-layouts: 14.1 us -> none  [the longest x1 7.05 us: correlate(): fwd_sorted = jnp.take(forward, position, axis=1)]
    select_n x8 -> x0, other arithmetic: 12.1 us -> none  [the longest x1 7.59 us: correlate(): adj_sorted = jnp.take(adjoint, position, axis=1)]
    all_to_all x1 -> x0, starting transfers between devices: 8.8 us -> none  [from_everyone(): return lax.all_to_all(copies, axis, split_axis=0, concat_axis=0, tiled=True)]
    another operation x1 -> x0, local copies, waits for them, and re-layouts: 8.68 us -> none  [per_device(): field_source[0]]
  transfers between devices with their start and end apart: 8 -> 0, of which waited for: 7 -> 0; matrix products, arithmetic and copies ran while one was open for 6% -> 0% of each run, Pallas kernels for 0% -> 0%
where the time goes in v1:
time: 95.2 us; the launch traced here: 93.6 us
  Pallas kernels  88.7 us (93%)
  local copies, waits for them, and re-layouts  4.24 us (4%)
    pallas_call x1, Pallas kernels, per_device(): pl.pallas_call(functools.partial(kernel, layers, peers, 1.0 / math.sqrt(h...  88.7 us
    unnamed x10, local copies, waits for them, and re-layouts  4.24 us

profile of v1, /device:TPU:2, one launch (start us, length us, event | category | flops | bytes accessed | tf_op | source)
XLA Modules:
  0.0 93.6 jit_solution(5849292831208647874)
XLA Ops:
  0.6 0.0 copy-start
  0.6 0.9 %copy-done = bf16[1,2,32,2048]{3,2,1,0:T(8,128)(2,1)S(1)} copy-done((bf16[1,2,32,2048]{3,2,1,0:T(8,128)(2,1)S(1)}, bf16[1,2,32,2048]{3,2,1,0:T(8,128)(2,1)}, u32[]{:S(2)}) %copy-start) | copy-done | bytes 262168
  1.6 0.0 copy-start.1
  1.6 0.7 copy-done.1
  2.3 0.0 copy-start.2
  2.3 0.7 copy-done.2
  3.0 0.0 copy-start.3
  3.0 0.7 copy-done.3
  3.7 88.7 %shard_map.59 = (f32[1,2,64]{2,1,0:T(2,128)S(1)}, bf16[1,2,32,128]{3,2,1,0:T(8,128)(2,1)S(1)}) custom-call(bf16[2,32,128]{2,1,0:T(8,128)(2,1)S(1)} %copy-done.1, bf16[1,2,32,2048]{3,2,1,0:T(8,128)(2,1)S(1)} %copy-done, bf16[1,2,32,128]{3,2,1,0:T(8,128)(2,1)S(1)} %copy-done.2, s32[1,2048]{1,0:T(1,128)S(1)} %bitcast.1), custom_call_target="tpu_custom_call" | custom-call | tf_op jit(solution)/shard_map/pallas_call | solution.py:184
  92.4 0.6 copy.8
  93.0 0.6 copy.9
Async XLA Ops:
  0.6 1.0 %copy-start = (bf16[1,2,32,2048]{3,2,1,0:T(8,128)(2,1)S(1)}, bf16[1,2,32,2048]{3,2,1,0:T(8,128)(2,1)}, u32[]{:S(2)}) copy-start(bf16[1,2,32,2048]{3,2,1,0:T(8,128)(2,1)} %transfer_ref.1) | copy-start | bytes 786436
  1.6 0.7 copy-start.1
  2.3 0.7 copy-start.2
  3.0 0.7 copy-start.3

commit v2 on v1

v2 whole, which is shorter than its diff:
```python
import functools
import math

import jax
import jax.numpy as jnp
from jax import lax
from jax.experimental import pallas as pl
from jax.experimental.pallas import tpu as pltpu
from jax.sharding import PartitionSpec as P

MESH = pl.DeviceIdType.MESH
F32 = jnp.float32
BF16 = jnp.bfloat16
MATES = 4


def kernel(
    layers, peers, scale,
    source_hbm, transfer_hbm, fields_hbm, orders_hbm, grads_ref, bound_ref,
    source, fields, orders, rows_all, adj, fwd, flat, hot_fwd, hot_adj, lined, factor,
    packed_src, packed_fld, outgoing, landed, partial, gathered,
    load_sem, send_sem, rows_sem, adj_sem, fwd_sem, land_sem, part_sem,
):
    group = lax.axis_index("layer")
    me = lax.axis_index("harm")
    mate = me % MATES
    clan = me // MATES
    clans = peers // MATES
    rows = source.shape[1]
    half = rows // 2
    cols = source.shape[2]
    slice_b = cols // MATES
    harm = rows * peers
    band = 2 * rows
    depth = min(256, harm)
    steps = harm // depth
    top = layers - 1

    loads = [
        pltpu.make_async_copy(source_hbm, source, load_sem.at[0]),
        pltpu.make_async_copy(orders_hbm, orders, load_sem.at[1]),
        pltpu.make_async_copy(fields_hbm.at[0], fields, load_sem.at[2]),
        pltpu.make_async_copy(transfer_hbm.at[0], rows_all.at[mate], load_sem.at[3]),
    ]
    for load in loads:
        load.start()

    barrier = pltpu.get_barrier_semaphore()
    with jax.named_scope("signal"):

        @pl.loop(1, peers)
        def _(j):
            pl.semaphore_signal(
                barrier, inc=1, device_id=(group, lax.rem(me + j, peers)), device_id_type=MESH
            )

        @pl.when(group < top)
        def _():
            above = jnp.minimum(group + 1, top)

            @pl.loop(0, clans)
            def _(j):
                pl.semaphore_signal(
                    barrier, inc=1, device_id=(above, j * MATES + mate), device_id_type=MESH
                )

    lane = lax.broadcasted_iota(jnp.int32, (1, cols), 1)
    in_slice = lax.rem(lane, 2 * slice_b)

    def pack(block, into):
        value = block[...].astype(F32)
        for m in range(MATES):
            parts = []
            for where in range(4):
                plane, upper = where % 2, where // 2
                piece = value[plane, upper * half : (upper + 1) * half, :]
                shift = (where - m) * slice_b % cols
                parts.append(pltpu.roll(piece, shift, 1) if shift else piece)
            tile = parts[3]
            for where in range(2, -1, -1):
                tile = jnp.where(lane < (where + 1) * slice_b, parts[where], tile)
            into[m] = tile.astype(BF16)

    with jax.named_scope("pack"):
        loads[0].wait()
        pack(source, packed_src)
        loads[2].wait()
        pack(fields, packed_fld)
        loads[1].wait()

    border = harm - 16
    chunk = min(256, harm)
    tall = harm + 16
    part = 688 if tall % 688 == 0 else tall

    with jax.named_scope("hots"):
        lined[pl.ds(0, border), :] = jnp.zeros((border, cols), BF16)
        lined[pl.ds(2 * harm, harm), :] = jnp.zeros((harm, cols), BF16)

    def build_fwd():
        @pl.loop(0, harm // chunk)
        def _(r):
            index = lax.broadcasted_iota(jnp.int32, (chunk, depth), 0)
            order = r * chunk + (index // band) * band + (band - 1) - index % band
            for k in range(steps):
                hit = orders[:, pl.ds(k * depth, depth)] == order
                hot_fwd[pl.ds(pl.multiple_of(r * chunk, chunk), chunk), pl.ds(k * depth, depth)] = (
                    jnp.where(hit, 1.0, 0.0).astype(BF16)
                )

    def build_adj():
        @pl.loop(0, tall // part)
        def _(r):
            order = r * part - 15 + lax.broadcasted_iota(jnp.int32, (part, depth), 0)

            @pl.loop(0, steps)
            def _(k):
                at = pl.ds(pl.multiple_of(k * depth, depth), depth)
                hot_adj[pl.ds(pl.multiple_of(r * part, 16), part), at] = (
                    jnp.where(orders[:, at] == order, 1.0, 0.0).astype(BF16)
                )

    with jax.named_scope("hots"):
        build_fwd()

    with jax.named_scope("barrier"):

        @pl.when(group > 0)
        def _():
            pl.semaphore_wait(barrier, peers - 1 + clans)

        @pl.when(group == 0)
        def _():
            pl.semaphore_wait(barrier, peers - 1)

    def remote(src, dst, sem, arrived, target, index):
        return pltpu.make_async_remote_copy(
            src_ref=src, dst_ref=dst, send_sem=send_sem.at[sem], recv_sem=arrived,
            device_id=(target, index), device_id_type=MESH,
        )

    def wait_for(buffer, count, sem):
        part_of = buffer.at[pl.ds(0, count)]
        pltpu.make_async_copy(part_of, part_of, sem).wait()

    def to_mates(sources, dst, sem, arrived):
        for j in range(1, MATES):
            other = lax.rem(mate + j, MATES)
            src = sources(other)
            remote(src, dst.at[mate], sem, arrived, group, clan * MATES + other).start()

    def scatter(tiles, dst, sem, arrived):
        @pl.loop(1, peers)
        def _(j):
            index = lax.rem(me + j, peers)
            remote(tiles.at[lax.rem(index, MATES)], dst.at[me], sem, arrived, group, index).start()

        dst[me] = tiles[mate]

    def send_fields():
        with jax.named_scope("sendf"):
            scatter(packed_fld, fwd, 2, fwd_sem)

    loads[3].wait()
    with jax.named_scope("spread"):
        to_mates(lambda other: rows_all.at[mate], rows_all, 0, rows_sem)

        @pl.when(group == top)
        def _():
            scatter(packed_src, adj, 1, adj_sem)

        @pl.when(group < top)
        def _():
            send_fields()

    def unpack(tiles, into):
        count = depth // rows
        for k in range(steps):
            value = tiles[pl.ds(k * count, count)].astype(F32)
            turned = pltpu.roll(value.reshape(count * half, cols), cols // 2, 1).reshape(value.shape)
            lower = jnp.where(lane < cols // 2, value, turned)
            upper = jnp.where(lane < cols // 2, turned, value)
            both = jnp.concatenate([lower, upper], axis=1).reshape(depth, cols)
            into[pl.ds(k * depth, depth), :] = both.astype(BF16)

    def propagate():
        with jax.named_scope("propagate"):
            unpack(adj, flat)
            total = jnp.zeros((MATES * 2 * rows, cols), F32)
            for k in range(steps):
                at = pl.ds(k * depth, depth)
                matrix = rows_all[:, :, :, at].reshape(MATES * 2 * rows, depth)
                total += jnp.dot(matrix, flat[at, :], preferred_element_type=F32)
            total = total.reshape(MATES, 2, rows, cols)
            cross = pltpu.roll(total[:, 1].reshape(MATES * rows, cols), slice_b, 1)
            cross = cross.reshape(MATES, rows, cols)
            result = total[:, 0] + jnp.where(in_slice < slice_b, -cross, cross)
            outgoing[...] = jnp.where(lane < cols // 2, result[:, :half], result[:, half:]).astype(BF16)

        with jax.named_scope("forward"):

            @pl.when(group > 0)
            def _():
                below = jnp.maximum(group - 1, 0)

                @pl.loop(0, clans)
                def _(j):
                    index = lax.rem(clan + j, clans) * MATES + mate
                    remote(
                        outgoing, adj.at[pl.ds(clan * MATES, MATES)], 3, adj_sem, below, index
                    ).start()

            landed[mate] = outgoing[mate]
            to_mates(lambda other: outgoing.at[other], landed, 4, land_sem)

    @pl.when(group == top)
    def _():
        with jax.named_scope("wait_t"):
            wait_for(rows_all, MATES - 1, rows_sem)
        with jax.named_scope("wait_a"):
            wait_for(adj, peers - 1, adj_sem)
        propagate()
        send_fields()

    with jax.named_scope("hots"):
        build_adj()

    with jax.named_scope("wait_f"):
        wait_for(fwd, peers - 1, fwd_sem)
    with jax.named_scope("sortf"):
        unpack(fwd, flat)
        sign = jnp.where(in_slice < slice_b, 1.0, -1.0)
        quads = chunk // band

        @pl.loop(0, harm // chunk)
        def _(r):
            at = pl.ds(pl.multiple_of(r * chunk, chunk), chunk)
            total = jnp.zeros((chunk, cols), F32)
            for k in range(steps):
                total += jnp.dot(
                    hot_fwd[at, pl.ds(k * depth, depth)], flat[pl.ds(k * depth, depth), :],
                    preferred_element_type=F32,
                )
            real = total * sign
            imag = pltpu.roll(total, slice_b, 1)
            for pair in range(quads // 2):
                lo, mid, hi = 2 * pair * band, (2 * pair + 1) * band, (2 * pair + 2) * band
                upper = jnp.where(lane < cols // 2, real[lo:mid], real[mid:hi])
                lower = jnp.where(lane < cols // 2, imag[lo:mid], imag[mid:hi])
                turned = jnp.concatenate([upper, lower], axis=0).T
                factor[r, pl.ds(pair * cols, cols), :] = turned.astype(BF16)

    @pl.when(group < top)
    def _():
        with jax.named_scope("wait_t"):
            wait_for(rows_all, MATES - 1, rows_sem)
        with jax.named_scope("wait_a"):
            wait_for(adj, peers, adj_sem)
        propagate()

    @pl.when(group == top)
    def _():
        unpack(adj, flat)

    with jax.named_scope("sorta"):

        @pl.loop(0, tall // part)
        def _(r):
            at = pl.ds(pl.multiple_of(r * part, 16), part)
            total = jnp.zeros((part, cols), F32)
            for k in range(steps):
                total += jnp.dot(
                    hot_adj[at, pl.ds(k * depth, depth)], flat[pl.ds(k * depth, depth), :],
                    preferred_element_type=F32,
                )
            lined[pl.ds(pl.multiple_of(border + r * part, 16), part), :] = total.astype(BF16)

    with jax.named_scope("gram"):
        quad = chunk // band
        tall_window = (MATES + 1) * band
        gram = jnp.zeros((tall_window, 2 * band), F32)
        for n in range(harm // chunk):
            start = (MATES * clan + quad * n) * band

            def window(m):
                return lined[pl.ds(pl.multiple_of(start + m * band, band), tall_window), :]

            left = jnp.concatenate(
                [
                    jnp.where(lane < cols // 2, window(2 * pair), window(2 * pair + 1))
                    for pair in range(quad // 2)
                ],
                axis=1,
            )
            gram += jnp.dot(left, factor[n], preferred_element_type=F32)
        for m in range(MATES):
            turned = pltpu.roll(gram[m * band : (m + 2) * band].T, band + 1, 1, stride=1, stride_axis=0)
            real = jnp.sum(turned[:band], axis=0, keepdims=True)
            imag = jnp.sum(turned[band:], axis=0, keepdims=True)
            partial[m] = jnp.where(lane < band, real, imag)

    with jax.named_scope("reduce"):
        gathered[mate] = partial[mate]
        to_mates(lambda other: partial.at[other], gathered, 5, part_sem)

    with jax.named_scope("land"):
        wait_for(landed, MATES - 1, land_sem)
        pieces = [landed[m].astype(F32) for m in range(MATES)]
        for plane in range(2):
            for upper in range(2):
                where = 2 * upper + plane
                tile = None
                for m in range(MATES):
                    shift = (m - where) * slice_b % cols
                    moved = pltpu.roll(pieces[m], shift, 1) if shift else pieces[m]
                    tile = moved if m == 0 else jnp.where(lane < m * slice_b, tile, moved)
                bound_ref[0, plane, pl.ds(upper * half, half), :] = tile.astype(BF16)

    with jax.named_scope("sum"):
        wait_for(gathered, MATES - 1, part_sem)
        total = gathered[0]
        for m in range(1, MATES):
            total = total + gathered[m]
        total = total * scale
        grads_ref[0, 0:1, :] = total[:, :band]
        grads_ref[0, 1:2, :] = total[:, band:]

    with jax.named_scope("drain"):
        wait_for(rows_all, MATES - 1, send_sem.at[0])
        wait_for(fwd, peers - 1, send_sem.at[2])
        wait_for(landed, MATES - 1, send_sem.at[4])
        wait_for(gathered, MATES - 1, send_sem.at[5])

        @pl.when(group == top)
        def _():
            wait_for(adj, peers - 1, send_sem.at[1])

        @pl.when(group > 0)
        def _():
            wait_for(adj, peers, send_sem.at[3])


def solution(mesh):
    layers, peers = mesh.shape["layer"], mesh.shape["harm"]

    def per_device(source, transfer, fields, orders):
        rows, cols = source.shape[1], source.shape[2]
        harm = rows * peers
        band = 2 * rows
        chunk = min(256, harm)
        vmem = pl.BlockSpec(memory_space=pltpu.VMEM)
        hbm = pl.BlockSpec(memory_space=pltpu.HBM)
        tile = (rows // 2, cols)
        return pl.pallas_call(
            functools.partial(kernel, layers, peers, 1.0 / math.sqrt(harm * cols)),
            out_shape=(
                jax.ShapeDtypeStruct((1, 2, band), F32),
                jax.ShapeDtypeStruct((1, 2, rows, cols), BF16),
            ),
            in_specs=[hbm] * 4,
            out_specs=(vmem, vmem),
            scratch_shapes=[
                pltpu.VMEM((2, rows, cols), BF16),
                pltpu.VMEM((2, rows, cols), BF16),
                pltpu.VMEM((1, harm), jnp.int32),
                pltpu.VMEM((MATES, 2, rows, harm), BF16),
                pltpu.VMEM((peers, *tile), BF16),
                pltpu.VMEM((peers, *tile), BF16),
                pltpu.VMEM((harm, cols), BF16),
                pltpu.VMEM((harm, harm), BF16),
                pltpu.VMEM((harm + 16, harm), BF16),
                pltpu.VMEM((3 * harm, cols), BF16),
                pltpu.VMEM((harm // chunk, chunk // band * 2 * (cols // MATES), 2 * band), BF16),
                pltpu.VMEM((MATES, *tile), BF16),
                pltpu.VMEM((MATES, *tile), BF16),
                pltpu.VMEM((MATES, *tile), BF16),
                pltpu.VMEM((MATES, *tile), BF16),
                pltpu.VMEM((MATES, 1, cols), F32),
                pltpu.VMEM((MATES, 1, cols), F32),
                pltpu.SemaphoreType.DMA((4,)),
                pltpu.SemaphoreType.DMA((6,)),
                pltpu.SemaphoreType.DMA,
                pltpu.SemaphoreType.DMA,
                pltpu.SemaphoreType.DMA,
                pltpu.SemaphoreType.DMA,
                pltpu.SemaphoreType.DMA,
            ],
            compiler_params=pltpu.CompilerParams(
                collective_id=0, has_side_effects=True, vmem_limit_bytes=56 * 1024 * 1024
            ),
        )(source, transfer, fields, orders.reshape(1, harm))

    return jax.shard_map(
        per_device,
        mesh=mesh,
        in_specs=(
            P(None, "harm", None),
            P("layer", None, "harm", None),
            P("layer", None, "harm", None),
            P(),
        ),
        out_specs=(P("layer", None, "harm"), P("layer", None, "harm", None)),
        check_vma=False,
    )
```

time: 95.2 us -> 60.3 us (0.63); the launches traced: 93.6 us -> 60.1 us
  Pallas kernels: 88.7 us -> 56.9 us
  local copies, waits for them, and re-layouts: 4.24 us -> 2.54 us
    pallas_call x1, Pallas kernels: 88.7 us -> 56.9 us  [per_device(): pl.pallas_call(functools.partial(kernel, layers, peers, 1.0 / math.sqrt(h...]
    unnamed x10 -> x4, local copies, waits for them, and re-layouts: 4.24 us -> 2.54 us
where the time goes in v2:
time: 60.3 us; the launch traced here: 60.1 us
  Pallas kernels  56.9 us (94%)
  local copies, waits for them, and re-layouts  2.54 us (4%)
  between operations  0.65 us (1%)
    pallas_call x1, Pallas kernels, per_device(): pl.pallas_call(functools.partial(kernel, layers, peers, 1.0 / math.sqrt(h...  56.9 us
    unnamed x4, local copies, waits for them, and re-layouts  2.54 us

profile of v2, /device:TPU:2, one launch (start us, length us, event | category | flops | bytes accessed | tf_op | source)
XLA Modules:
  0.0 60.1 jit_solution(16906524542859091098)
XLA Ops:
  0.6 56.9 %shard_map.59 = (f32[1,2,64]{2,1,0:T(2,128)}, bf16[1,2,32,128]{3,2,1,0:T(8,128)(2,1)}) custom-call(bf16[2,32,128]{2,1,0:T(8,128)(2,1)} %source_hbm.1, bf16[1,2,32,2048]{3,2,1,0:T(8,128)(2,1)} %transfer_hbm.1, bf16[1,2,32,128]{3,2,1,0:T(8,128)(2,1)} %fields_hbm.1, s32[1,2048]{1,0:T(1,128)} %bitcast.1), custom_call_target="tpu_custom_call" | custom-call | tf_op jit(solution)/shard_map/pallas_call | solution.py:354
  57.5 0.0 copy-start
  57.5 0.7 %copy-done = f32[1,2,64]{2,1,0:T(2,128)S(1)} copy-done((f32[1,2,64]{2,1,0:T(2,128)S(1)}, f32[1,2,64]{2,1,0:T(2,128)}, u32[]{:S(2)}) %copy-start) | copy-done | bytes 536
  58.2 0.6 copy.8
  58.7 1.3 %copy.9 = bf16[1,2,32,128]{3,2,1,0:T(8,128)(2,1)} copy(bf16[1,2,32,128]{3,2,1,0:T(8,128)(2,1)} %get-tuple-element.5) | data formatting | bytes 32768
Async XLA Ops:
  57.5 0.7 %copy-start = (f32[1,2,64]{2,1,0:T(2,128)S(1)}, f32[1,2,64]{2,1,0:T(2,128)}, u32[]{:S(2)}) copy-start(f32[1,2,64]{2,1,0:T(2,128)} %get-tuple-element.4) | copy-start | bytes 1540

commit v3 on v2

v3 whole, which is shorter than its diff:
```python
import functools
import math

import jax
import jax.numpy as jnp
from jax import lax
from jax.experimental import pallas as pl
from jax.experimental.pallas import tpu as pltpu
from jax.sharding import PartitionSpec as P

MESH = pl.DeviceIdType.MESH
F32 = jnp.float32
BF16 = jnp.bfloat16
MATES = 4
LINES = 4


def kernel(
    layers, peers, scale,
    source_hbm, transfer_hbm, fields_hbm, orders_hbm, grads_ref, bound_ref,
    source, fields, orders, rows_all, adj, fwd, flat, stretched, hot_fwd, hot_adj, lined, factor,
    packed_src, packed_fld, stage_src, stage_fld, outgoing, landed, partial, gathered, sorting,
    load_sem, send_sem, rows_sem, adj_sem, fwd_sem, stage_sem, land_sem, part_sem, clear_sem, go_sem,
):
    group = lax.axis_index("layer")
    me = lax.axis_index("harm")
    mate = me % MATES
    clan = me // MATES
    clans = peers // MATES
    lines = min(LINES, clans)
    planes = clans // lines
    line = clan % lines
    plane_at = clan // lines
    rows = source.shape[1]
    half = rows // 2
    cols = source.shape[2]
    slice_b = cols // MATES
    harm = rows * peers
    band = 2 * rows
    depth = min(256, harm)
    steps = harm // depth
    top = layers - 1
    clan_rows = MATES * rows
    share = planes * clan_rows

    loads = [
        pltpu.make_async_copy(transfer_hbm.at[0], rows_all.at[mate], load_sem.at[3]),
        pltpu.make_async_copy(source_hbm, source, load_sem.at[0]),
        pltpu.make_async_copy(fields_hbm.at[0], fields, load_sem.at[2]),
        pltpu.make_async_copy(orders_hbm, orders, load_sem.at[1]),
    ]
    for load in loads:
        load.start()

    barrier = pltpu.get_barrier_semaphore()

    def mate_index(j):
        return clan * MATES + lax.rem(mate + j, MATES)

    def clan_index(far_line, far_plane):
        other = lax.rem(plane_at + far_plane, planes) * lines + lax.rem(line + far_line, lines)
        return other * MATES + mate

    def by_distance(size):
        return sorted(range(size), key=lambda d: -min(d, size - d))

    offsets = [(a, b) for a in by_distance(lines) for b in by_distance(planes)]

    with jax.named_scope("signal"):
        for a, b in offsets[:-1]:
            pl.semaphore_signal(
                barrier, inc=1, device_id=(group, clan_index(a, b)), device_id_type=MESH
            )
        for j in (2, 1, 3):
            pl.semaphore_signal(barrier, inc=1, device_id=(group, mate_index(j)), device_id_type=MESH)

        @pl.when(group > 0)
        def _():
            pl.semaphore_signal(
                barrier, inc=1, device_id=(jnp.maximum(group - 1, 0), me), device_id_type=MESH
            )

    lane = lax.broadcasted_iota(jnp.int32, (1, cols), 1)
    in_slice = lax.rem(lane, 2 * slice_b)

    def pack(block, into):
        value = block[...].astype(F32)
        for m in range(MATES):
            parts = []
            for where in range(4):
                plane, upper = where % 2, where // 2
                piece = value[plane, upper * half : (upper + 1) * half, :]
                shift = (where - m) * slice_b % cols
                parts.append(pltpu.roll(piece, shift, 1) if shift else piece)
            tile = parts[3]
            for where in range(2, -1, -1):
                tile = jnp.where(lane < (where + 1) * slice_b, parts[where], tile)
            into[m] = tile.astype(BF16)

    border = harm - 16
    chunk = min(256, harm)
    tall = harm + 16
    part = 688 if tall % 688 == 0 else tall

    with jax.named_scope("pack"):
        loads[1].wait()
        pack(source, packed_src)
        loads[2].wait()
        pack(fields, packed_fld)
        lined[pl.ds(0, border), :] = jnp.zeros((border, cols), BF16)
        lined[pl.ds(2 * harm, harm), :] = jnp.zeros((harm, cols), BF16)
        loads[3].wait()
        loads[0].wait()

    def build_fwd():
        with jax.named_scope("hotf"):

            @pl.loop(0, harm // chunk)
            def _(r):
                index = lax.broadcasted_iota(jnp.int32, (chunk, depth), 0)
                order = r * chunk + (index // band) * band + (band - 1) - index % band
                for k in range(steps):
                    hit = orders[:, pl.ds(k * depth, depth)] == order
                    hot_fwd[
                        pl.ds(pl.multiple_of(r * chunk, chunk), chunk), pl.ds(k * depth, depth)
                    ] = jnp.where(hit, 1.0, 0.0).astype(BF16)

    def build_adj():
        with jax.named_scope("hota"):

            @pl.loop(0, tall // part)
            def _(r):
                order = r * part - 15 + lax.broadcasted_iota(jnp.int32, (part, clan_rows), 0)

                @pl.loop(0, clans)
                def _(k):
                    at = pl.ds(pl.multiple_of(k * clan_rows, clan_rows), clan_rows)
                    to = (k % lines) * planes + k // lines
                    to = pl.ds(pl.multiple_of(to * clan_rows, clan_rows), clan_rows)
                    hot_adj[pl.ds(pl.multiple_of(r * part, 16), part), to] = (
                        jnp.where(orders[:, at] == order, 1.0, 0.0).astype(BF16)
                    )

    with jax.named_scope("barrier"):

        @pl.when(group < top)
        def _():
            pl.semaphore_wait(barrier, clans - 1 + MATES)
            pl.semaphore_signal(
                clear_sem, inc=1, device_id=(jnp.minimum(group + 1, top), me), device_id_type=MESH
            )

        @pl.when(group == top)
        def _():
            pl.semaphore_wait(barrier, clans - 1 + MATES - 1)

    def remote(src, dst, sem, arrived, target, index):
        return pltpu.make_async_remote_copy(
            src_ref=src, dst_ref=dst, send_sem=send_sem.at[sem], recv_sem=arrived,
            device_id=(target, index), device_id_type=MESH,
        )

    def wait_for(buffer, count, sem):
        part_of = buffer.at[pl.ds(0, count)]
        pltpu.make_async_copy(part_of, part_of, sem).wait()

    def to_mates(tiles, dst, sem, arrived):
        for j in (2, 1, 3):
            other = lax.rem(mate + j, MATES)
            remote(
                tiles.at[other], dst.at[mate], sem, arrived, group, clan * MATES + other
            ).start()
        dst[mate] = tiles[mate]

    clan_tiles = pl.ds(clan * MATES, MATES)

    def to_clans(tiles, dst, sem, arrived, target, everyone):
        for a, b in offsets if everyone else offsets[:-1]:
            remote(tiles, dst.at[clan_tiles], sem, arrived, target, clan_index(a, b)).start()

    right, left = mate_index(1), mate_index(MATES - 1)
    from_left, from_right = lax.rem(mate + MATES - 1, MATES), lax.rem(mate + 1, MATES)

    def start_rows():
        for first in (0, 1):
            to_right = rows_all.at[mate, first]
            to_left = rows_all.at[mate, 1 - first]
            remote(to_right, to_right, 0, rows_sem.at[2 * first], group, right).start()
            remote(to_left, to_left, 0, rows_sem.at[2 * first + 1], group, left).start()

    def wait_half(sem):
        wait_for(rows_all.at[0], 1, rows_sem.at[sem])

    def relay_rows():
        with jax.named_scope("relay_t"):
            wait_half(0)
            block = rows_all.at[from_left, 0]
            remote(block, block, 1, rows_sem.at[4], group, right).start()
            wait_half(1)
            block = rows_all.at[from_right, 1]
            remote(block, block, 1, rows_sem.at[5], group, left).start()

    def wait_rows():
        with jax.named_scope("wait_t"):
            for k in (2, 3, 4, 5):
                wait_half(k)

    def start_fields():
        to_mates(packed_fld, stage_fld, 2, stage_sem.at[0])

    def relay_fields():
        with jax.named_scope("relay_f"):
            wait_for(stage_fld, MATES - 1, stage_sem.at[0])
            to_clans(stage_fld, fwd, 3, fwd_sem, group, False)
            fwd[clan_tiles] = stage_fld[...]

    with jax.named_scope("spread"):

        @pl.when(group == top)
        def _():
            to_mates(packed_src, stage_src, 4, stage_sem.at[1])
            start_rows()
            with jax.named_scope("relay_s"):
                wait_for(stage_src, MATES - 1, stage_sem.at[1])
                to_clans(stage_src, adj, 5, adj_sem.at[line], top, False)
                adj[clan_tiles] = stage_src[...]
            relay_rows()
            pl.semaphore_wait(clear_sem, 1)
            pl.semaphore_signal(go_sem, inc=1, device_id=(top - 1, me), device_id_type=MESH)

        @pl.when(group == top - 1)
        def _():
            build_fwd()
            build_adj()
            with jax.named_scope("wait_go"):
                pl.semaphore_wait(go_sem, 1)
            start_fields()
            start_rows()
            relay_fields()
            relay_rows()

        @pl.when(group < top - 1)
        def _():
            build_fwd()
            build_adj()
            start_fields()
            start_rows()
            relay_fields()
            relay_rows()

    def unpack(tiles):
        count = tiles.shape[0]
        value = tiles.astype(F32)
        turned = pltpu.roll(value.reshape(count * half, cols), cols // 2, 1).reshape(value.shape)
        lower = jnp.where(lane < cols // 2, value, turned)
        upper = jnp.where(lane < cols // 2, turned, value)
        return jnp.concatenate([lower, upper], axis=1).reshape(count * rows, cols).astype(BF16)

    def sort_share(far, first, last):
        z = lax.rem(line + far, lines)
        at = pl.ds(pl.multiple_of(z * share, share), share)

        @pl.loop(0, tall // part)
        def _(r):
            here = pl.ds(pl.multiple_of(r * part, 16), part)
            total = jnp.dot(hot_adj[here, at], flat[at, :], preferred_element_type=F32)
            if not first:
                total += sorting[here, :]
            if last:
                lined[pl.ds(pl.multiple_of(border + r * part, 16), part), :] = total.astype(BF16)
            else:
                sorting[here, :] = total

    near_first = by_distance(lines)[::-1]

    def receive(sort):
        total = jnp.zeros((MATES * 2 * rows, cols), F32)
        for step, far in enumerate(near_first):
            z = lax.rem(line + far, lines)
            with jax.named_scope("wait_a%d" % step):
                if step == 0:

                    @pl.when(group == top)
                    def _():
                        wait_for(adj, MATES * (planes - 1), adj_sem.at[z])

                    @pl.when(group < top)
                    def _():
                        wait_for(adj, MATES * planes, adj_sem.at[z])
                else:
                    wait_for(adj, MATES * planes, adj_sem.at[z])
            with jax.named_scope("propagate"):
                blocks = [adj[pl.ds((p * lines + z) * MATES, MATES)] for p in range(planes)]
                right_side = unpack(jnp.concatenate(blocks, axis=0))
                flat[pl.ds(pl.multiple_of(z * share, share), share), :] = right_side
                matrix = jnp.concatenate(
                    [
                        rows_all[
                            :, :, :, pl.ds(pl.multiple_of((p * lines + z) * clan_rows, clan_rows), clan_rows)
                        ].reshape(MATES * 2 * rows, clan_rows)
                        for p in range(planes)
                    ],
                    axis=1,
                )
                total += jnp.dot(matrix, right_side, preferred_element_type=F32)
            last = step == lines - 1
            if last:
                with jax.named_scope("forward"):
                    total = total.reshape(MATES, 2, rows, cols)
                    cross = pltpu.roll(total[:, 1].reshape(MATES * rows, cols), slice_b, 1)
                    cross = cross.reshape(MATES, rows, cols)
                    result = total[:, 0] + jnp.where(in_slice < slice_b, -cross, cross)
                    outgoing[...] = jnp.where(
                        lane < cols // 2, result[:, :half], result[:, half:]
                    ).astype(BF16)
                    if not sort:
                        below = jnp.maximum(group - 1, 0)

                        @pl.when(group < top)
                        def _():
                            pl.semaphore_wait(clear_sem, 1)

                        to_clans(outgoing, adj, 6, adj_sem.at[line], below, True)
                    to_mates(outgoing, landed, 7, land_sem)
            if sort:
                with jax.named_scope("sort0"):
                    sort_share(far, step == 0, last)

    @pl.when(group >= top - 1)
    def _():
        wait_rows()
        receive(False)

    @pl.when(group == top)
    def _():
        start_fields()
        build_fwd()
        relay_fields()
        build_adj()

    with jax.named_scope("wait_f"):
        wait_for(fwd, peers - MATES, fwd_sem)
    with jax.named_scope("sortf"):
        for k in range(steps):
            count = depth // rows
            flat_fwd = unpack(fwd[pl.ds(k * count, count)])
            stretched[pl.ds(k * depth, depth), :] = flat_fwd
        sign = jnp.where(in_slice < slice_b, 1.0, -1.0)
        quads = chunk // band

        @pl.loop(0, harm // chunk)
        def _(r):
            at = pl.ds(pl.multiple_of(r * chunk, chunk), chunk)
            total = jnp.zeros((chunk, cols), F32)
            for k in range(steps):
                total += jnp.dot(
                    hot_fwd[at, pl.ds(k * depth, depth)], stretched[pl.ds(k * depth, depth), :],
                    preferred_element_type=F32,
                )
            real = total * sign
            imag = pltpu.roll(total, slice_b, 1)
            for pair in range(quads // 2):
                lo, mid, hi = 2 * pair * band, (2 * pair + 1) * band, (2 * pair + 2) * band
                upper = jnp.where(lane < cols // 2, real[lo:mid], real[mid:hi])
                lower = jnp.where(lane < cols // 2, imag[lo:mid], imag[mid:hi])
                turned = jnp.concatenate([upper, lower], axis=0).T
                factor[r, pl.ds(pair * cols, cols), :] = turned.astype(BF16)

    @pl.when(group == 1)
    def _():
        wait_rows()
        receive(False)

    @pl.when(group == 0)
    def _():
        wait_rows()
        receive(True)

    @pl.when(group > 0)
    def _():
        with jax.named_scope("sorta"):
            for step, far in enumerate(near_first):
                sort_share(far, step == 0, step == lines - 1)

    with jax.named_scope("gram"):
        quad = chunk // band
        tall_window = (MATES + 1) * band
        gram = jnp.zeros((tall_window, 2 * band), F32)
        for n in range(harm // chunk):
            start = (MATES * clan + quad * n) * band

            def window(m):
                return lined[pl.ds(pl.multiple_of(start + m * band, band), tall_window), :]

            left = jnp.concatenate(
                [
                    jnp.where(lane < cols // 2, window(2 * pair), window(2 * pair + 1))
                    for pair in range(quad // 2)
                ],
                axis=1,
            )
            gram += jnp.dot(left, factor[n], preferred_element_type=F32)
        for m in range(MATES):
            turned = pltpu.roll(gram[m * band : (m + 2) * band].T, band + 1, 1, stride=1, stride_axis=0)
            real = jnp.sum(turned[:band], axis=0, keepdims=True)
            imag = jnp.sum(turned[band:], axis=0, keepdims=True)
            partial[m] = jnp.where(lane < band, real, imag)

    with jax.named_scope("reduce"):
        to_mates(partial, gathered, 8, part_sem)

    with jax.named_scope("land"):
        wait_for(landed, MATES - 1, land_sem)
        pieces = [landed[m].astype(F32) for m in range(MATES)]
        for plane in range(2):
            for upper in range(2):
                where = 2 * upper + plane
                tile = None
                for m in range(MATES):
                    shift = (m - where) * slice_b % cols
                    moved = pltpu.roll(pieces[m], shift, 1) if shift else pieces[m]
                    tile = moved if m == 0 else jnp.where(lane < m * slice_b, tile, moved)
                bound_ref[0, plane, pl.ds(upper * half, half), :] = tile.astype(BF16)

    with jax.named_scope("sum"):
        wait_for(gathered, MATES - 1, part_sem)
        total = gathered[0]
        for m in range(1, MATES):
            total = total + gathered[m]
        total = total * scale
        grads_ref[0, 0:1, :] = total[:, :band]
        grads_ref[0, 1:2, :] = total[:, band:]

    with jax.named_scope("drain"):
        wait_for(rows_all, 2, send_sem.at[0])
        wait_for(rows_all, 1, send_sem.at[1])
        wait_for(stage_fld, MATES - 1, send_sem.at[2])
        wait_for(fwd, peers - MATES, send_sem.at[3])
        wait_for(landed, MATES - 1, send_sem.at[7])
        wait_for(gathered, MATES - 1, send_sem.at[8])

        @pl.when(group == top)
        def _():
            wait_for(stage_src, MATES - 1, send_sem.at[4])
            wait_for(adj, peers - MATES, send_sem.at[5])

        @pl.when(group > 0)
        def _():
            wait_for(adj, peers, send_sem.at[6])


def solution(mesh):
    layers, peers = mesh.shape["layer"], mesh.shape["harm"]

    def per_device(source, transfer, fields, orders):
        rows, cols = source.shape[1], source.shape[2]
        harm = rows * peers
        band = 2 * rows
        chunk = min(256, harm)
        vmem = pl.BlockSpec(memory_space=pltpu.VMEM)
        hbm = pl.BlockSpec(memory_space=pltpu.HBM)
        tile = (rows // 2, cols)
        return pl.pallas_call(
            functools.partial(kernel, layers, peers, 1.0 / math.sqrt(harm * cols)),
            out_shape=(
                jax.ShapeDtypeStruct((1, 2, band), F32),
                jax.ShapeDtypeStruct((1, 2, rows, cols), BF16),
            ),
            in_specs=[hbm] * 4,
            out_specs=(vmem, vmem),
            scratch_shapes=[
                pltpu.VMEM((2, rows, cols), BF16),
                pltpu.VMEM((2, rows, cols), BF16),
                pltpu.VMEM((1, harm), jnp.int32),
                pltpu.VMEM((MATES, 2, rows, harm), BF16),
                pltpu.VMEM((peers, *tile), BF16),
                pltpu.VMEM((peers, *tile), BF16),
                pltpu.VMEM((harm, cols), BF16),
                pltpu.VMEM((harm, cols), BF16),
                pltpu.VMEM((harm, harm), BF16),
                pltpu.VMEM((harm + 16, harm), BF16),
                pltpu.VMEM((3 * harm, cols), BF16),
                pltpu.VMEM((harm // chunk, chunk // band * 2 * (cols // MATES), 2 * band), BF16),
                *[pltpu.VMEM((MATES, *tile), BF16)] * 6,
                pltpu.VMEM((MATES, 1, cols), F32),
                pltpu.VMEM((MATES, 1, cols), F32),
                pltpu.VMEM((harm + 16, cols), F32),
                pltpu.SemaphoreType.DMA((4,)),
                pltpu.SemaphoreType.DMA((9,)),
                pltpu.SemaphoreType.DMA((6,)),
                pltpu.SemaphoreType.DMA((LINES,)),
                pltpu.SemaphoreType.DMA,
                pltpu.SemaphoreType.DMA((2,)),
                pltpu.SemaphoreType.DMA,
                pltpu.SemaphoreType.DMA,
                pltpu.SemaphoreType.REGULAR,
                pltpu.SemaphoreType.REGULAR,
            ],
            compiler_params=pltpu.CompilerParams(
                collective_id=0, has_side_effects=True, vmem_limit_bytes=44 * 1024 * 1024
            ),
        )(
            *(
                pltpu.with_memory_space_constraint(value, pltpu.HBM)
                for value in (source, transfer, fields, orders.reshape(1, harm))
            )
        )

    return jax.shard_map(
        per_device,
        mesh=mesh,
        in_specs=(
            P(None, "harm", None),
            P("layer", None, "harm", None),
            P("layer", None, "harm", None),
            P(),
        ),
        out_specs=(P("layer", None, "harm"), P("layer", None, "harm", None)),
        check_vma=False,
    )
```

time: 60.3 us -> 50.2 us (0.83)
  Pallas kernels: 56.9 us -> 48.3 us
  local copies, waits for them, and re-layouts: 2.54 us -> 1.17 us
    pallas_call x1, Pallas kernels: 56.9 us -> 48.3 us  [per_device(): pl.pallas_call(functools.partial(kernel, layers, peers, 1.0 / math.sqrt(h...]
    unnamed x4 -> x2, local copies, waits for them, and re-layouts: 2.54 us -> 1.17 us
where the time goes in v3:
time: 50.2 us; the launch traced here: 50.1 us
  Pallas kernels  48.3 us (96%)
  local copies, waits for them, and re-layouts  1.17 us (2%)
  between operations  0.64 us (1%)
    pallas_call x1, Pallas kernels, per_device(): pl.pallas_call(functools.partial(kernel, layers, peers, 1.0 / math.sqrt(h...  48.3 us
    unnamed x2, local copies, waits for them, and re-layouts  1.17 us

profile of v3, /device:TPU:2, one launch (start us, length us, event | category | flops | bytes accessed | tf_op | source)
XLA Modules:
  0.0 50.1 jit_solution(4228984136523629850)
XLA Ops:
  0.6 48.3 %shard_map.59 = (f32[1,2,64]{2,1,0:T(2,128)S(1)}, bf16[1,2,32,128]{3,2,1,0:T(8,128)(2,1)S(1)}) custom-call(bf16[2,32,128]{2,1,0:T(8,128)(2,1)} %source_hbm.1, bf16[1,2,32,2048]{3,2,1,0:T(8,128)(2,1)} %transfer_hbm.1, bf16[1,2,32,128]{3,2,1,0:T(8,128)(2,1)} %fields_hbm.1, s32[1,2048]{1,0:T(1,128)} %bitcast.1), custom_call_target="tpu_custom_call" | custom-call | tf_op jit(solution)/shard_map/pallas_call | solution.py:463
  49.0 0.6 %copy.8 = f32[1,2,64]{2,1,0:T(2,128)} copy(f32[1,2,64]{2,1,0:T(2,128)S(1)} %get-tuple-element.4) | data formatting | bytes 1024
  49.5 0.6 %copy.9 = bf16[1,2,32,128]{3,2,1,0:T(8,128)(2,1)} copy(bf16[1,2,32,128]{3,2,1,0:T(8,128)(2,1)S(1)} %get-tuple-element.5) | data formatting | bytes 32768

commit v4 on v3

--- a/solution.py
+++ b/solution.py
@@ -18,9 +18,10 @@
 def kernel(
     layers, peers, scale,
     source_hbm, transfer_hbm, fields_hbm, orders_hbm, grads_ref, bound_ref,
-    source, fields, orders, rows_all, adj, fwd, flat, stretched, hot_fwd, hot_adj, lined, factor,
+    source, fields, orders, rows_all, adj, fwd, stretched, column, hot_fwd, hot_adj, lined, shifted, factor,
     packed_src, packed_fld, stage_src, stage_fld, outgoing, landed, partial, gathered, sorting,
     load_sem, send_sem, rows_sem, adj_sem, fwd_sem, stage_sem, land_sem, part_sem, clear_sem, go_sem,
+    line_sem, plane_sem,
 ):
     group = lax.axis_index("layer")
     me = lax.axis_index("harm")
@@ -57,22 +58,23 @@
     def mate_index(j):
         return clan * MATES + lax.rem(mate + j, MATES)
 
+    def place(plane, line_of):
+        return (plane * lines + line_of) * MATES + mate
+
     def clan_index(far_line, far_plane):
-        other = lax.rem(plane_at + far_plane, planes) * lines + lax.rem(line + far_line, lines)
-        return other * MATES + mate
+        return place(lax.rem(plane_at + far_plane, planes), lax.rem(line + far_line, lines))
 
     def by_distance(size):
         return sorted(range(size), key=lambda d: -min(d, size - d))
 
     offsets = [(a, b) for a in by_distance(lines) for b in by_distance(planes)]
 
+    near_lines = [place(plane_at, lax.rem(line + far, lines)) for far in (1, lines - 1)]
+    near_planes = [place(lax.rem(plane_at + far, planes), line) for far in (2, 1, 3)]
+
     with jax.named_scope("signal"):
-        for a, b in offsets[:-1]:
-            pl.semaphore_signal(
-                barrier, inc=1, device_id=(group, clan_index(a, b)), device_id_type=MESH
-            )
-        for j in (2, 1, 3):
-            pl.semaphore_signal(barrier, inc=1, device_id=(group, mate_index(j)), device_id_type=MESH)
+        for index in near_lines + near_planes + [mate_index(j) for j in (2, 1, 3)]:
+            pl.semaphore_signal(barrier, inc=1, device_id=(group, index), device_id_type=MESH)
 
         @pl.when(group > 0)
         def _():
@@ -97,18 +99,18 @@
                 tile = jnp.where(lane < (where + 1) * slice_b, parts[where], tile)
             into[m] = tile.astype(BF16)
 
-    border = harm - 16
+    border = harm - cols
+    wide = harm + 2 * cols
     chunk = min(256, harm)
-    tall = harm + 16
-    part = 688 if tall % 688 == 0 else tall
 
     with jax.named_scope("pack"):
         loads[1].wait()
         pack(source, packed_src)
         loads[2].wait()
         pack(fields, packed_fld)
-        lined[pl.ds(0, border), :] = jnp.zeros((border, cols), BF16)
-        lined[pl.ds(2 * harm, harm), :] = jnp.zeros((harm, cols), BF16)
+        for buffer in (lined, shifted):
+            buffer[:, pl.ds(0, border)] = jnp.zeros((2 * slice_b, border), BF16)
+            buffer[:, pl.ds(border + wide, border)] = jnp.zeros((2 * slice_b, border), BF16)
         loads[3].wait()
         loads[0].wait()
 
@@ -127,32 +129,47 @@
 
     def build_adj():
         with jax.named_scope("hota"):
-
-            @pl.loop(0, tall // part)
-            def _(r):
-                order = r * part - 15 + lax.broadcasted_iota(jnp.int32, (part, clan_rows), 0)
-
-                @pl.loop(0, clans)
-                def _(k):
-                    at = pl.ds(pl.multiple_of(k * clan_rows, clan_rows), clan_rows)
-                    to = (k % lines) * planes + k // lines
-                    to = pl.ds(pl.multiple_of(to * clan_rows, clan_rows), clan_rows)
-                    hot_adj[pl.ds(pl.multiple_of(r * part, 16), part), to] = (
-                        jnp.where(orders[:, at] == order, 1.0, 0.0).astype(BF16)
-                    )
+            for k in range(harm // cols):
+                row = orders[:, pl.ds(k * cols, cols)].astype(F32)
+                column[pl.ds(k * cols, cols), :] = jnp.broadcast_to(row, (cols, cols)).T
+
+            @pl.loop(0, peers)
+            def _(tile):
+                owner = tile // MATES
+                spot = (owner // lines) * MATES + tile % MATES
+                for upper in range(2):
+                    order = column[pl.ds(pl.multiple_of(tile * rows + upper * half, half), half), :]
+                    row = (owner % lines) * share + upper * (share // 2) + spot * half
+                    row = pl.ds(pl.multiple_of(row, half), half)
+                    for k in range(wide // cols):
+                        want = (lane + (k * cols - cols + 1)).astype(F32)
+                        hot_adj[row, pl.ds(k * cols, cols)] = jnp.where(order == want, 1.0, 0.0).astype(BF16)
 
     with jax.named_scope("barrier"):
 
         @pl.when(group < top)
         def _():
-            pl.semaphore_wait(barrier, clans - 1 + MATES)
-            pl.semaphore_signal(
-                clear_sem, inc=1, device_id=(jnp.minimum(group + 1, top), me), device_id_type=MESH
-            )
+            pl.semaphore_wait(barrier, len(near_lines) + len(near_planes) + MATES)
 
         @pl.when(group == top)
         def _():
-            pl.semaphore_wait(barrier, clans - 1 + MATES - 1)
+            pl.semaphore_wait(barrier, len(near_lines) + len(near_planes) + MATES - 1)
+
+        for index in near_lines:
+            pl.semaphore_signal(line_sem, inc=1, device_id=(group, index), device_id_type=MESH)
+
+    def all_here():
+        with jax.named_scope("here"):
+            pl.semaphore_wait(line_sem, len(near_lines))
+            for index in near_planes:
+                pl.semaphore_signal(plane_sem, inc=1, device_id=(group, index), device_id_type=MESH)
+            pl.semaphore_wait(plane_sem, len(near_planes))
+
+            @pl.when(group < top)
+            def _():
+                pl.semaphore_signal(
+                    clear_sem, inc=1, device_id=(jnp.minimum(group + 1, top), me), device_id_type=MESH
+                )
 
     def remote(src, dst, sem, arrived, target, index):
         return pltpu.make_async_remote_copy(
@@ -220,6 +237,7 @@
         def _():
             to_mates(packed_src, stage_src, 4, stage_sem.at[1])
             start_rows()
+            all_here()
             with jax.named_scope("relay_s"):
                 wait_for(stage_src, MATES - 1, stage_sem.at[1])
                 to_clans(stage_src, adj, 5, adj_sem.at[line], top, False)
@@ -230,6 +248,7 @@
 
         @pl.when(group == top - 1)
         def _():
+            all_here()
             build_fwd()
             build_adj()
             with jax.named_scope("wait_go"):
@@ -241,6 +260,7 @@
 
         @pl.when(group < top - 1)
         def _():
+            all_here()
             build_fwd()
             build_adj()
             start_fields()
@@ -258,18 +278,35 @@
 
     def sort_share(far, first, last):
         z = lax.rem(line + far, lines)
+        tiles = jnp.concatenate(
+            [adj[pl.ds((p * lines + z) * MATES, MATES)].reshape(MATES * half, cols) for p in range(planes)],
+            axis=0,
+        )
+        turned = tiles.astype(F32).T.astype(BF16)
+        left = jnp.concatenate([turned[: cols // 2], turned[cols // 2 :]], axis=1)
         at = pl.ds(pl.multiple_of(z * share, share), share)
-
-        @pl.loop(0, tall // part)
-        def _(r):
-            here = pl.ds(pl.multiple_of(r * part, 16), part)
-            total = jnp.dot(hot_adj[here, at], flat[at, :], preferred_element_type=F32)
+        span = 3 * depth if wide % (3 * depth) == 0 else wide
+        tail = None
+        for k in reversed(range(wide // span)):
+            here = pl.ds(k * span, span)
+            total = jnp.dot(left, hot_adj[at, here], preferred_element_type=F32)
             if not first:
-                total += sorting[here, :]
-            if last:
-                lined[pl.ds(pl.multiple_of(border + r * part, 16), part), :] = total.astype(BF16)
-            else:
-                sorting[here, :] = total
+                total += sorting[:, here]
+            if not last:
+                sorting[:, here] = total
+                continue
+            lined[:, pl.ds(border + k * span, span)] = total.astype(BF16)
+            pieces = [
+                pltpu.roll(total[:, i * cols : (i + 1) * cols], cols // 2, 1) for i in range(span // cols)
+            ]
+            pieces.append(jnp.zeros_like(pieces[0]) if tail is None else tail)
+            tail = pieces[0]
+            for i in range(span // cols):
+                shifted[:, pl.ds(border + k * span + i * cols, cols)] = jnp.where(
+                    lane < cols // 2, pieces[i], pieces[i + 1]
+                ).astype(BF16)
+        if last:
+            shifted[:, pl.ds(border - cols, cols)] = jnp.where(lane < cols // 2, 0.0, tail).astype(BF16)
 
     near_first = by_distance(lines)[::-1]
 
@@ -292,7 +329,6 @@
             with jax.named_scope("propagate"):
                 blocks = [adj[pl.ds((p * lines + z) * MATES, MATES)] for p in range(planes)]
                 right_side = unpack(jnp.concatenate(blocks, axis=0))
-                flat[pl.ds(pl.multiple_of(z * share, share), share), :] = right_side
                 matrix = jnp.concatenate(
                     [
                         rows_all[
@@ -363,8 +399,8 @@
                 lo, mid, hi = 2 * pair * band, (2 * pair + 1) * band, (2 * pair + 2) * band
                 upper = jnp.where(lane < cols // 2, real[lo:mid], real[mid:hi])
                 lower = jnp.where(lane < cols // 2, imag[lo:mid], imag[mid:hi])
-                turned = jnp.concatenate([upper, lower], axis=0).T
-                factor[r, pl.ds(pair * cols, cols), :] = turned.astype(BF16)
+                both = jnp.concatenate([upper, lower], axis=0)
+                factor[r, :, pl.ds(pair * cols, cols)] = both.astype(BF16)
 
     @pl.when(group == 1)
     def _():
@@ -384,24 +420,23 @@
 
     with jax.named_scope("gram"):
         quad = chunk // band
-        tall_window = (MATES + 1) * band
-        gram = jnp.zeros((tall_window, 2 * band), F32)
+        view = (MATES + 2) * band
+        gram = jnp.zeros((2 * band, view), F32)
         for n in range(harm // chunk):
             start = (MATES * clan + quad * n) * band
-
-            def window(m):
-                return lined[pl.ds(pl.multiple_of(start + m * band, band), tall_window), :]
-
-            left = jnp.concatenate(
-                [
-                    jnp.where(lane < cols // 2, window(2 * pair), window(2 * pair + 1))
-                    for pair in range(quad // 2)
-                ],
-                axis=1,
-            )
-            gram += jnp.dot(left, factor[n], preferred_element_type=F32)
+            window = []
+            for k in range(quad):
+                buffer = shifted if k % 2 else lined
+                at = pl.ds(pl.multiple_of(start + (k - k % 2) * band, 2 * band), view)
+                window.append(buffer[:, at])
+            gram += jnp.dot(factor[n], jnp.concatenate(window, axis=0), preferred_element_type=F32)
         for m in range(MATES):
-            turned = pltpu.roll(gram[m * band : (m + 2) * band].T, band + 1, 1, stride=1, stride_axis=0)
+            if m % 2:
+                both = gram[:, (m - 1) * band : (m + 3) * band]
+                turned = pltpu.roll(both, 2 * band + 1, 1, stride=1, stride_axis=0)[:, : 2 * band]
+            else:
+                both = gram[:, m * band : (m + 2) * band]
+                turned = pltpu.roll(both, band + 1, 1, stride=1, stride_axis=0)
             real = jnp.sum(turned[:band], axis=0, keepdims=True)
             imag = jnp.sum(turned[band:], axis=0, keepdims=True)
             partial[m] = jnp.where(lane < band, real, imag)
@@ -476,15 +511,16 @@
                 pltpu.VMEM((peers, *tile), BF16),
                 pltpu.VMEM((peers, *tile), BF16),
                 pltpu.VMEM((harm, cols), BF16),
-                pltpu.VMEM((harm, cols), BF16),
+                pltpu.VMEM((harm, cols), F32),
                 pltpu.VMEM((harm, harm), BF16),
-                pltpu.VMEM((harm + 16, harm), BF16),
-                pltpu.VMEM((3 * harm, cols), BF16),
-                pltpu.VMEM((harm // chunk, chunk // band * 2 * (cols // MATES), 2 * band), BF16),
+                pltpu.VMEM((harm, harm + 2 * cols), BF16),
+                pltpu.VMEM((2 * cols // MATES, 3 * harm), BF16),
+                pltpu.VMEM((2 * cols // MATES, 3 * harm), BF16),
+                pltpu.VMEM((harm // chunk, 2 * band, chunk // band * 2 * (cols // MATES)), BF16),
                 *[pltpu.VMEM((MATES, *tile), BF16)] * 6,
                 pltpu.VMEM((MATES, 1, cols), F32),
                 pltpu.VMEM((MATES, 1, cols), F32),
-                pltpu.VMEM((harm + 16, cols), F32),
+                pltpu.VMEM((2 * cols // MATES, harm + 2 * cols), F32),
                 pltpu.SemaphoreType.DMA((4,)),
                 pltpu.SemaphoreType.DMA((9,)),
                 pltpu.SemaphoreType.DMA((6,)),
@@ -493,8 +529,7 @@
                 pltpu.SemaphoreType.DMA((2,)),
                 pltpu.SemaphoreType.DMA,
                 pltpu.SemaphoreType.DMA,
-                pltpu.SemaphoreType.REGULAR,
-                pltpu.SemaphoreType.REGULAR,
+                *[pltpu.SemaphoreType.REGULAR] * 4,
             ],
             compiler_params=pltpu.CompilerParams(
                 collective_id=0, has_side_effects=True, vmem_limit_bytes=44 * 1024 * 1024

time: 50.2 us -> 48.3 us (0.962)
  Pallas kernels: 48.3 us -> 46.4 us
    pallas_call x1, Pallas kernels: 48.3 us -> 46.4 us  [per_device(): pl.pallas_call(functools.partial(kernel, layers, peers, 1.0 / math.sqrt(h...]
where the time goes in v4:
time: 48.3 us; the launch traced here: 48.2 us
  Pallas kernels  46.4 us (96%)
  local copies, waits for them, and re-layouts  1.17 us (2%)
  between operations  0.64 us (1%)
    pallas_call x1, Pallas kernels, per_device(): pl.pallas_call(functools.partial(kernel, layers, peers, 1.0 / math.sqrt(h...  46.4 us
    unnamed x2, local copies, waits for them, and re-layouts  1.17 us

profile of v4, /device:TPU:2, one launch (start us, length us, event | category | flops | bytes accessed | tf_op | source)
XLA Modules:
  0.0 48.2 jit_solution(12749494847730163084)
XLA Ops:
  0.6 46.4 %shard_map.59 = (f32[1,2,64]{2,1,0:T(2,128)S(1)}, bf16[1,2,32,128]{3,2,1,0:T(8,128)(2,1)S(1)}) custom-call(bf16[2,32,128]{2,1,0:T(8,128)(2,1)} %source_hbm.1, bf16[1,2,32,2048]{3,2,1,0:T(8,128)(2,1)} %transfer_hbm.1, bf16[1,2,32,128]{3,2,1,0:T(8,128)(2,1)} %fields_hbm.1, s32[1,2048]{1,0:T(1,128)} %bitcast.1), custom_call_target="tpu_custom_call" | custom-call | tf_op jit(solution)/shard_map/pallas_call | solution.py:498
  47.0 0.6 %copy.8 = f32[1,2,64]{2,1,0:T(2,128)} copy(f32[1,2,64]{2,1,0:T(2,128)S(1)} %get-tuple-element.4) | data formatting | bytes 1024
  47.6 0.6 %copy.9 = bf16[1,2,32,128]{3,2,1,0:T(8,128)(2,1)} copy(bf16[1,2,32,128]{3,2,1,0:T(8,128)(2,1)S(1)} %get-tuple-element.5) | data formatting | bytes 32768

commit v5 on v4

--- a/solution.py
+++ b/solution.py
@@ -41,6 +41,8 @@
     depth = min(256, harm)
     steps = harm // depth
     top = layers - 1
+    helper = top - 2
+    far_line = lines // 2
     clan_rows = MATES * rows
     share = planes * clan_rows
 
@@ -80,6 +82,12 @@
         def _():
             pl.semaphore_signal(
                 barrier, inc=1, device_id=(jnp.maximum(group - 1, 0), me), device_id_type=MESH
+            )
+
+        @pl.when(group == top)
+        def _():
+            pl.semaphore_signal(
+                barrier, inc=1, device_id=(helper, clan_index(far_line, 0)), device_id_type=MESH
             )
 
     lane = lax.broadcasted_iota(jnp.int32, (1, cols), 1)
@@ -147,23 +155,32 @@
 
     with jax.named_scope("barrier"):
 
-        @pl.when(group < top)
-        def _():
-            pl.semaphore_wait(barrier, len(near_lines) + len(near_planes) + MATES)
+        close = len(near_lines) + len(near_planes) + MATES - 1
+
+        @pl.when((group < top) & (group != helper))
+        def _():
+            pl.semaphore_wait(barrier, close + 1)
+
+        @pl.when(group == helper)
+        def _():
+            pl.semaphore_wait(barrier, close + 2)
 
         @pl.when(group == top)
         def _():
-            pl.semaphore_wait(barrier, len(near_lines) + len(near_planes) + MATES - 1)
-
-        for index in near_lines:
-            pl.semaphore_signal(line_sem, inc=1, device_id=(group, index), device_id_type=MESH)
+            pl.semaphore_wait(barrier, close)
+
+        for index in near_planes:
+            pl.semaphore_signal(plane_sem, inc=1, device_id=(group, index), device_id_type=MESH)
+
+    def near_here():
+        with jax.named_scope("near"):
+            pl.semaphore_wait(plane_sem, len(near_planes))
+            for index in near_lines:
+                pl.semaphore_signal(line_sem, inc=1, device_id=(group, index), device_id_type=MESH)
 
     def all_here():
         with jax.named_scope("here"):
             pl.semaphore_wait(line_sem, len(near_lines))
-            for index in near_planes:
-                pl.semaphore_signal(plane_sem, inc=1, device_id=(group, index), device_id_type=MESH)
-            pl.semaphore_wait(plane_sem, len(near_planes))
 
             @pl.when(group < top)
             def _():
@@ -191,8 +208,8 @@
 
     clan_tiles = pl.ds(clan * MATES, MATES)
 
-    def to_clans(tiles, dst, sem, arrived, target, everyone):
-        for a, b in offsets if everyone else offsets[:-1]:
+    def to_clans(tiles, dst, sem, arrived, target, to):
+        for a, b in to:
             remote(tiles, dst.at[clan_tiles], sem, arrived, target, clan_index(a, b)).start()
 
     right, left = mate_index(1), mate_index(MATES - 1)
@@ -228,45 +245,62 @@
     def relay_fields():
         with jax.named_scope("relay_f"):
             wait_for(stage_fld, MATES - 1, stage_sem.at[0])
-            to_clans(stage_fld, fwd, 3, fwd_sem, group, False)
+            to_clans(stage_fld, fwd, 3, fwd_sem, group, offsets[:-1])
             fwd[clan_tiles] = stage_fld[...]
 
     with jax.named_scope("spread"):
+
+        near = [offset for offset in offsets[:-1] if offset[0] != far_line]
+        far = [offset for offset in offsets if offset[0] == far_line]
+
+        def relay_source(to):
+            with jax.named_scope("relay_s"):
+                wait_for(stage_src, MATES - 1, stage_sem.at[1])
+                to_clans(stage_src, adj, 5, adj_sem.at[line], top, to)
 
         @pl.when(group == top)
         def _():
             to_mates(packed_src, stage_src, 4, stage_sem.at[1])
             start_rows()
+            near_here()
+            relay_source(near)
+            adj[clan_tiles] = stage_src[...]
+            relay_rows()
             all_here()
-            with jax.named_scope("relay_s"):
-                wait_for(stage_src, MATES - 1, stage_sem.at[1])
-                to_clans(stage_src, adj, 5, adj_sem.at[line], top, False)
-                adj[clan_tiles] = stage_src[...]
-            relay_rows()
             pl.semaphore_wait(clear_sem, 1)
             pl.semaphore_signal(go_sem, inc=1, device_id=(top - 1, me), device_id_type=MESH)
 
         @pl.when(group == top - 1)
         def _():
+            near_here()
             all_here()
-            build_fwd()
-            build_adj()
             with jax.named_scope("wait_go"):
                 pl.semaphore_wait(go_sem, 1)
             start_fields()
             start_rows()
+            build_fwd()
+            relay_rows()
+            build_adj()
+
+        @pl.when(group < top - 1)
+        def _():
+            @pl.when(group == helper)
+            def _():
+                to_mates(packed_src, stage_src, 4, stage_sem.at[1])
+
+            near_here()
+
+            @pl.when(group == helper)
+            def _():
+                relay_source(far)
+
+            all_here()
+            start_fields()
+            start_rows()
+            build_fwd()
             relay_fields()
             relay_rows()
-
-        @pl.when(group < top - 1)
-        def _():
-            all_here()
-            build_fwd()
             build_adj()
-            start_fields()
-            start_rows()
-            relay_fields()
-            relay_rows()
 
     def unpack(tiles):
         count = tiles.shape[0]
@@ -356,13 +390,13 @@
                         def _():
                             pl.semaphore_wait(clear_sem, 1)
 
-                        to_clans(outgoing, adj, 6, adj_sem.at[line], below, True)
+                        to_clans(outgoing, adj, 6, adj_sem.at[line], below, offsets)
                     to_mates(outgoing, landed, 7, land_sem)
             if sort:
                 with jax.named_scope("sort0"):
                     sort_share(far, step == 0, last)
 
-    @pl.when(group >= top - 1)
+    @pl.when(group > 0)
     def _():
         wait_rows()
         receive(False)
@@ -371,8 +405,11 @@
     def _():
         start_fields()
         build_fwd()
+        build_adj()
+
+    @pl.when(group >= top - 1)
+    def _():
         relay_fields()
-        build_adj()
 
     with jax.named_scope("wait_f"):
         wait_for(fwd, peers - MATES, fwd_sem)
@@ -401,11 +438,6 @@
                 lower = jnp.where(lane < cols // 2, imag[lo:mid], imag[mid:hi])
                 both = jnp.concatenate([upper, lower], axis=0)
                 factor[r, :, pl.ds(pair * cols, cols)] = both.astype(BF16)
-
-    @pl.when(group == 1)
-    def _():
-        wait_rows()
-        receive(False)
 
     @pl.when(group == 0)
     def _():
@@ -474,10 +506,17 @@
         wait_for(landed, MATES - 1, send_sem.at[7])
         wait_for(gathered, MATES - 1, send_sem.at[8])
 
+        @pl.when(group == helper)
+        def _():
+            wait_for(adj, MATES * len(far), send_sem.at[5])
+
+        @pl.when((group == top) | (group == helper))
+        def _():
+            wait_for(stage_src, MATES - 1, send_sem.at[4])
+
         @pl.when(group == top)
         def _():
-            wait_for(stage_src, MATES - 1, send_sem.at[4])
-            wait_for(adj, peers - MATES, send_sem.at[5])
+            wait_for(adj, MATES * len(near), send_sem.at[5])
 
         @pl.when(group > 0)
         def _():

time: 48.3 us -> 45.1 us (0.934)
  Pallas kernels: 46.4 us -> 43.1 us
    pallas_call x1, Pallas kernels: 46.4 us -> 43.1 us  [per_device(): pl.pallas_call(functools.partial(kernel, layers, peers, 1.0 / math.sqrt(h...]
where the time goes in v5:
time: 45.1 us; the launch traced here: 44.9 us
  Pallas kernels  43.1 us (96%)
  local copies, waits for them, and re-layouts  1.17 us (3%)
  between operations  0.64 us (1%)
    pallas_call x1, Pallas kernels, per_device(): pl.pallas_call(functools.partial(kernel, layers, peers, 1.0 / math.sqrt(h...  43.1 us
    unnamed x2, local copies, waits for them, and re-layouts  1.17 us

profile of v5, /device:TPU:2, one launch (start us, length us, event | category | flops | bytes accessed | tf_op | source)
XLA Modules:
  0.0 44.9 jit_solution(14979005745853206280)
XLA Ops:
  0.6 43.1 %shard_map.59 = (f32[1,2,64]{2,1,0:T(2,128)S(1)}, bf16[1,2,32,128]{3,2,1,0:T(8,128)(2,1)S(1)}) custom-call(bf16[2,32,128]{2,1,0:T(8,128)(2,1)} %source_hbm.1, bf16[1,2,32,2048]{3,2,1,0:T(8,128)(2,1)} %transfer_hbm.1, bf16[1,2,32,128]{3,2,1,0:T(8,128)(2,1)} %fields_hbm.1, s32[1,2048]{1,0:T(1,128)} %bitcast.1), custom_call_target="tpu_custom_call" | custom-call | tf_op jit(solution)/shard_map/pallas_call | solution.py:537
  43.7 0.6 %copy.8 = f32[1,2,64]{2,1,0:T(2,128)} copy(f32[1,2,64]{2,1,0:T(2,128)S(1)} %get-tuple-element.4) | data formatting | bytes 1024
  44.3 0.6 %copy.9 = bf16[1,2,32,128]{3,2,1,0:T(8,128)(2,1)} copy(bf16[1,2,32,128]{3,2,1,0:T(8,128)(2,1)S(1)} %get-tuple-element.5) | data formatting | bytes 32768

commit v6 on v5

--- a/solution.py
+++ b/solution.py
@@ -18,10 +18,9 @@
 def kernel(
     layers, peers, scale,
     source_hbm, transfer_hbm, fields_hbm, orders_hbm, grads_ref, bound_ref,
-    source, fields, orders, rows_all, adj, fwd, stretched, column, hot_fwd, hot_adj, lined, shifted, factor,
-    packed_src, packed_fld, stage_src, stage_fld, outgoing, landed, partial, gathered, sorting,
-    load_sem, send_sem, rows_sem, adj_sem, fwd_sem, stage_sem, land_sem, part_sem, clear_sem, go_sem,
-    line_sem, plane_sem,
+    source, fields, orders, rows_own, rows_all, rows_two, adj, adj_two, fwd, stretched, column, hot_fwd, hot_adj, lined, shifted, factor, factor_two,
+    packed_src, packed_fld, stage_src, stage_fld, outgoing, outgoing_two, landed, partial, partial_two, gathered, sorting,
+    load_sem, send_sem, rows_sem, adj_sem, two_sem, hand_sem, fwd_sem, stage_sem, land_sem, part_sem, clear_sem, line_sem, plane_sem, go_sem,
 ):
     group = lax.axis_index("layer")
     me = lax.axis_index("harm")
@@ -42,12 +41,14 @@
     steps = harm // depth
     top = layers - 1
     helper = top - 2
+    chain = (group == top) | (group == helper)
+    sibling = jnp.where(chain, jnp.maximum(group - 1, 0), jnp.minimum(group + 1, top))
     far_line = lines // 2
     clan_rows = MATES * rows
     share = planes * clan_rows
 
     loads = [
-        pltpu.make_async_copy(transfer_hbm.at[0], rows_all.at[mate], load_sem.at[3]),
+        pltpu.make_async_copy(transfer_hbm.at[0], rows_own, load_sem.at[3]),
         pltpu.make_async_copy(source_hbm, source, load_sem.at[0]),
         pltpu.make_async_copy(fields_hbm.at[0], fields, load_sem.at[2]),
         pltpu.make_async_copy(orders_hbm, orders, load_sem.at[1]),
@@ -78,14 +79,13 @@
         for index in near_lines + near_planes + [mate_index(j) for j in (2, 1, 3)]:
             pl.semaphore_signal(barrier, inc=1, device_id=(group, index), device_id_type=MESH)
 
-        @pl.when(group > 0)
-        def _():
-            pl.semaphore_signal(
-                barrier, inc=1, device_id=(jnp.maximum(group - 1, 0), me), device_id_type=MESH
-            )
+        @pl.when(chain)
+        def _():
+            pl.semaphore_signal(barrier, inc=1, device_id=(sibling, me), device_id_type=MESH)
 
         @pl.when(group == top)
         def _():
+            pl.semaphore_signal(barrier, inc=1, device_id=(helper, me), device_id_type=MESH)
             pl.semaphore_signal(
                 barrier, inc=1, device_id=(helper, clan_index(far_line, 0)), device_id_type=MESH
             )
@@ -120,7 +120,34 @@
             buffer[:, pl.ds(0, border)] = jnp.zeros((2 * slice_b, border), BF16)
             buffer[:, pl.ds(border + wide, border)] = jnp.zeros((2 * slice_b, border), BF16)
         loads[3].wait()
+
+    def arrange():
+        value = rows_own[...].reshape(2 * rows, harm)
+        count = harm // clan_rows
+        stacked = jnp.concatenate(
+            [value[:, k * clan_rows : (k + 1) * clan_rows] for k in range(count)], axis=0
+        )
+        at = lax.broadcasted_iota(jnp.int32, (clan_rows, 2 * clan_rows), 0)
+        to = lax.broadcasted_iota(jnp.int32, (clan_rows, 2 * clan_rows), 1)
+        inside = to % clan_rows
+        upper = (inside // (clan_rows // 2) + to // clan_rows) % 2
+        origin = inside % (clan_rows // 2) // half * rows + upper * half + inside % half
+        order = jnp.where(at == origin, 1.0, 0.0).astype(BF16)
+        moved = jnp.dot(stacked, order, preferred_element_type=F32)
+        moved = moved.reshape(count, 2, rows, 2 * clan_rows)
+        for z in range(lines):
+            for pair in range(planes // 2):
+                first = moved[2 * pair * lines + z]
+                second = moved[(2 * pair + 1) * lines + z]
+                lower = jnp.where(lane < cols // 2, first[:, :, :clan_rows], second[:, :, clan_rows:])
+                upper = jnp.where(lane < cols // 2, first[:, :, clan_rows:], second[:, :, :clan_rows])
+                start = z * share + pair * clan_rows
+                rows_all[mate, :, :, pl.ds(start, clan_rows)] = lower.astype(BF16)
+                rows_all[mate, :, :, pl.ds(start + share // 2, clan_rows)] = upper.astype(BF16)
+
+    with jax.named_scope("arrange"):
         loads[0].wait()
+        arrange()
 
     def build_fwd():
         with jax.named_scope("hotf"):
@@ -157,7 +184,7 @@
 
         close = len(near_lines) + len(near_planes) + MATES - 1
 
-        @pl.when((group < top) & (group != helper))
+        @pl.when(jnp.logical_not(chain))
         def _():
             pl.semaphore_wait(barrier, close + 1)
 
@@ -182,11 +209,13 @@
         with jax.named_scope("here"):
             pl.semaphore_wait(line_sem, len(near_lines))
 
-            @pl.when(group < top)
+            @pl.when(jnp.logical_not(chain))
             def _():
-                pl.semaphore_signal(
-                    clear_sem, inc=1, device_id=(jnp.minimum(group + 1, top), me), device_id_type=MESH
-                )
+                pl.semaphore_signal(clear_sem, inc=1, device_id=(sibling, me), device_id_type=MESH)
+
+            @pl.when(group == helper)
+            def _():
+                pl.semaphore_signal(clear_sem, inc=1, device_id=(top, me), device_id_type=MESH)
 
     def remote(src, dst, sem, arrived, target, index):
         return pltpu.make_async_remote_copy(
@@ -215,29 +244,39 @@
     right, left = mate_index(1), mate_index(MATES - 1)
     from_left, from_right = lax.rem(mate + MATES - 1, MATES), lax.rem(mate + 1, MATES)
 
-    def start_rows():
+    def start_rows(buffer, turn):
         for first in (0, 1):
-            to_right = rows_all.at[mate, first]
-            to_left = rows_all.at[mate, 1 - first]
-            remote(to_right, to_right, 0, rows_sem.at[2 * first], group, right).start()
-            remote(to_left, to_left, 0, rows_sem.at[2 * first + 1], group, left).start()
-
-    def wait_half(sem):
-        wait_for(rows_all.at[0], 1, rows_sem.at[sem])
-
-    def relay_rows():
-        with jax.named_scope("relay_t"):
-            wait_half(0)
-            block = rows_all.at[from_left, 0]
-            remote(block, block, 1, rows_sem.at[4], group, right).start()
-            wait_half(1)
-            block = rows_all.at[from_right, 1]
-            remote(block, block, 1, rows_sem.at[5], group, left).start()
-
-    def wait_rows():
-        with jax.named_scope("wait_t"):
+            to_right = buffer.at[mate, first]
+            to_left = buffer.at[mate, 1 - first]
+            for block, to, sem in ((to_right, right, 2 * first), (to_left, left, 2 * first + 1)):
+                remote(block, block, 9 * turn, rows_sem.at[6 * turn + sem], group, to).start()
+
+    def wait_half(turn, sem):
+        wait_for(rows_all.at[0], 1, rows_sem.at[6 * turn + sem])
+
+    def relay_rows(buffer, turn):
+        with jax.named_scope("relay_t%d" % turn):
+            wait_half(turn, 0)
+            block = buffer.at[from_left, 0]
+            remote(block, block, 9 * turn + 1, rows_sem.at[6 * turn + 4], group, right).start()
+            wait_half(turn, 1)
+            block = buffer.at[from_right, 1]
+            remote(block, block, 9 * turn + 1, rows_sem.at[6 * turn + 5], group, left).start()
+
+    def wait_rows(turn):
+        with jax.named_scope("wait_t%d" % turn):
             for k in (2, 3, 4, 5):
-                wait_half(k)
+                wait_half(turn, k)
+
+    def to_sibling(src, dst, sem, arrived):
+        remote(src, dst, sem, arrived, sibling, me).start()
+
+    def to_sibling_mates(tiles, dst, sem, arrived):
+        for j in (2, 1, 3, 0):
+            other = lax.rem(mate + j, MATES)
+            remote(
+                tiles.at[other], dst.at[mate], sem, arrived, sibling, clan * MATES + other
+            ).start()
 
     def start_fields():
         to_mates(packed_fld, stage_fld, 2, stage_sem.at[0])
@@ -261,46 +300,47 @@
         @pl.when(group == top)
         def _():
             to_mates(packed_src, stage_src, 4, stage_sem.at[1])
-            start_rows()
+            start_rows(rows_all, 0)
             near_here()
             relay_source(near)
             adj[clan_tiles] = stage_src[...]
-            relay_rows()
+            relay_rows(rows_all, 0)
+            wait_for(rows_all, 1, hand_sem.at[0])
+            start_rows(rows_two, 1)
             all_here()
+            pl.semaphore_wait(clear_sem, 2)
+
+        @pl.when(group == helper)
+        def _():
+            to_mates(packed_src, stage_src, 4, stage_sem.at[1])
+            near_here()
+            relay_source(far)
+            all_here()
+            start_fields()
+            start_rows(rows_all, 0)
+            build_fwd()
+            relay_fields()
+            relay_rows(rows_all, 0)
+            wait_for(rows_all, 1, hand_sem.at[0])
+            start_rows(rows_two, 1)
+            build_adj()
+            relay_rows(rows_two, 1)
             pl.semaphore_wait(clear_sem, 1)
-            pl.semaphore_signal(go_sem, inc=1, device_id=(top - 1, me), device_id_type=MESH)
-
-        @pl.when(group == top - 1)
-        def _():
+
+        @pl.when(jnp.logical_not(chain))
+        def _():
+            to_sibling(rows_all.at[mate], rows_two.at[mate], 11, hand_sem.at[0])
             near_here()
             all_here()
-            with jax.named_scope("wait_go"):
+            start_fields()
+            build_fwd()
+
+            @pl.when(group == top - 1)
+            def _():
+                build_adj()
                 pl.semaphore_wait(go_sem, 1)
-            start_fields()
-            start_rows()
-            build_fwd()
-            relay_rows()
-            build_adj()
-
-        @pl.when(group < top - 1)
-        def _():
-            @pl.when(group == helper)
-            def _():
-                to_mates(packed_src, stage_src, 4, stage_sem.at[1])
-
-            near_here()
-
-            @pl.when(group == helper)
-            def _():
-                relay_source(far)
-
-            all_here()
-            start_fields()
-            start_rows()
-            build_fwd()
+
             relay_fields()
-            relay_rows()
-            build_adj()
 
     def unpack(tiles):
         count = tiles.shape[0]
@@ -310,13 +350,15 @@
         upper = jnp.where(lane < cols // 2, turned, value)
         return jnp.concatenate([lower, upper], axis=1).reshape(count * rows, cols).astype(BF16)
 
-    def sort_share(far, first, last):
-        z = lax.rem(line + far, lines)
-        tiles = jnp.concatenate(
-            [adj[pl.ds((p * lines + z) * MATES, MATES)].reshape(MATES * half, cols) for p in range(planes)],
+    def share_tiles(tiles, z):
+        return jnp.concatenate(
+            [tiles[pl.ds((p * lines + z) * MATES, MATES)].reshape(MATES * half, cols) for p in range(planes)],
             axis=0,
         )
-        turned = tiles.astype(F32).T.astype(BF16)
+
+    def sort_share(tiles, far, first, last):
+        z = lax.rem(line + far, lines)
+        turned = share_tiles(tiles, z).astype(F32).T.astype(BF16)
         left = jnp.concatenate([turned[: cols // 2], turned[cols // 2 :]], axis=1)
         at = pl.ds(pl.multiple_of(z * share, share), share)
         span = 3 * depth if wide % (3 * depth) == 0 else wide
@@ -344,72 +386,71 @@
 
     near_first = by_distance(lines)[::-1]
 
-    def receive(sort):
-        total = jnp.zeros((MATES * 2 * rows, cols), F32)
+    def receive(tiles, block_rows, sems, own_there, out, sort):
+        lower = jnp.zeros((MATES * 2 * rows, cols), F32)
+        upper = jnp.zeros((MATES * 2 * rows, cols), F32)
         for step, far in enumerate(near_first):
             z = lax.rem(line + far, lines)
             with jax.named_scope("wait_a%d" % step):
-                if step == 0:
-
-                    @pl.when(group == top)
-                    def _():
-                        wait_for(adj, MATES * (planes - 1), adj_sem.at[z])
-
-                    @pl.when(group < top)
-                    def _():
-                        wait_for(adj, MATES * planes, adj_sem.at[z])
-                else:
-                    wait_for(adj, MATES * planes, adj_sem.at[z])
+                wait_for(tiles, MATES * (planes - (own_there and step == 0)), sems.at[z])
             with jax.named_scope("propagate"):
-                blocks = [adj[pl.ds((p * lines + z) * MATES, MATES)] for p in range(planes)]
-                right_side = unpack(jnp.concatenate(blocks, axis=0))
-                matrix = jnp.concatenate(
-                    [
-                        rows_all[
-                            :, :, :, pl.ds(pl.multiple_of((p * lines + z) * clan_rows, clan_rows), clan_rows)
-                        ].reshape(MATES * 2 * rows, clan_rows)
-                        for p in range(planes)
-                    ],
-                    axis=1,
+                packed = share_tiles(tiles, z)
+                at = pl.ds(pl.multiple_of(z * share, share), share // 2)
+                lower += jnp.dot(
+                    block_rows[:, :, :, at].reshape(MATES * 2 * rows, share // 2),
+                    packed, preferred_element_type=F32,
                 )
-                total += jnp.dot(matrix, right_side, preferred_element_type=F32)
+                at = pl.ds(pl.multiple_of(z * share + share // 2, share // 2), share // 2)
+                upper += jnp.dot(
+                    block_rows[:, :, :, at].reshape(MATES * 2 * rows, share // 2),
+                    packed, preferred_element_type=F32,
+                )
             last = step == lines - 1
             if last:
-                with jax.named_scope("forward"):
-                    total = total.reshape(MATES, 2, rows, cols)
-                    cross = pltpu.roll(total[:, 1].reshape(MATES * rows, cols), slice_b, 1)
-                    cross = cross.reshape(MATES, rows, cols)
-                    result = total[:, 0] + jnp.where(in_slice < slice_b, -cross, cross)
-                    outgoing[...] = jnp.where(
-                        lane < cols // 2, result[:, :half], result[:, half:]
-                    ).astype(BF16)
-                    if not sort:
-                        below = jnp.maximum(group - 1, 0)
-
-                        @pl.when(group < top)
-                        def _():
-                            pl.semaphore_wait(clear_sem, 1)
-
-                        to_clans(outgoing, adj, 6, adj_sem.at[line], below, offsets)
-                    to_mates(outgoing, landed, 7, land_sem)
+                mixed = jnp.where(lane < cols // 2, lower, upper)
+                total = mixed + pltpu.roll(mixed, cols // 2, 1)
+                total = total.reshape(MATES, 2, rows, cols)
+                cross = pltpu.roll(total[:, 1].reshape(MATES * rows, cols), slice_b, 1)
+                cross = cross.reshape(MATES, rows, cols)
+                result = total[:, 0] + jnp.where(in_slice < slice_b, -cross, cross)
+                out[...] = jnp.where(
+                    lane < cols // 2, result[:, :half], result[:, half:]
+                ).astype(BF16)
+                if sort:
+                    to_sibling_mates(out, landed, 13, land_sem)
             if sort:
                 with jax.named_scope("sort0"):
-                    sort_share(far, step == 0, last)
-
-    @pl.when(group > 0)
-    def _():
-        wait_rows()
-        receive(False)
+                    sort_share(tiles, far, step == 0, last)
+
+    def sort_all():
+        with jax.named_scope("sorta"):
+            for step, far in enumerate(near_first):
+                sort_share(adj, far, step == 0, step == lines - 1)
+
+    def first_layer():
+        with jax.named_scope("forward1"):
+            to_clans(outgoing, adj_two, 6, two_sem.at[line], group, offsets[:-1])
+            adj_two[clan_tiles] = outgoing[...]
+            to_mates(outgoing, landed, 7, land_sem)
 
     @pl.when(group == top)
     def _():
+        wait_rows(0)
+        receive(adj, rows_all, adj_sem, True, outgoing, False)
+        first_layer()
+        relay_rows(rows_two, 1)
         start_fields()
         build_fwd()
+        wait_rows(1)
+        pl.semaphore_signal(go_sem, inc=1, device_id=(sibling, me), device_id_type=MESH)
+        receive(adj_two, rows_two, two_sem, True, outgoing_two, False)
+        with jax.named_scope("forward2"):
+            to_clans(outgoing_two, adj, 12, adj_sem.at[line], helper, offsets)
+            to_sibling(adj_two, adj, 15, hand_sem.at[1])
+            to_sibling_mates(outgoing_two, landed, 13, land_sem)
+        relay_fields()
         build_adj()
-
-    @pl.when(group >= top - 1)
-    def _():
-        relay_fields()
+        sort_all()
 
     with jax.named_scope("wait_f"):
         wait_for(fwd, peers - MATES, fwd_sem)
@@ -439,45 +480,70 @@
                 both = jnp.concatenate([upper, lower], axis=0)
                 factor[r, :, pl.ds(pair * cols, cols)] = both.astype(BF16)
 
+    def correlate(made, into):
+        with jax.named_scope("gram"):
+            quad = chunk // band
+            view = (MATES + 2) * band
+            gram = jnp.zeros((2 * band, view), F32)
+            for n in range(harm // chunk):
+                start = (MATES * clan + quad * n) * band
+                window = []
+                for k in range(quad):
+                    buffer = shifted if k % 2 else lined
+                    at = pl.ds(pl.multiple_of(start + (k - k % 2) * band, 2 * band), view)
+                    window.append(buffer[:, at])
+                gram += jnp.dot(made[n], jnp.concatenate(window, axis=0), preferred_element_type=F32)
+            for m in range(MATES):
+                if m % 2:
+                    both = gram[:, (m - 1) * band : (m + 3) * band]
+                    turned = pltpu.roll(both, 2 * band + 1, 1, stride=1, stride_axis=0)[:, : 2 * band]
+                else:
+                    both = gram[:, m * band : (m + 2) * band]
+                    turned = pltpu.roll(both, band + 1, 1, stride=1, stride_axis=0)
+                real = jnp.sum(turned[:band], axis=0, keepdims=True)
+                imag = jnp.sum(turned[band:], axis=0, keepdims=True)
+                into[m] = jnp.where(lane < band, real, imag)
+
     @pl.when(group == 0)
     def _():
-        wait_rows()
-        receive(True)
+        to_sibling(factor, factor_two, 16, hand_sem.at[1])
+
+    @pl.when(group == top - 1)
+    def _():
+        with jax.named_scope("wait_adj"):
+            wait_for(adj, peers, hand_sem.at[1])
+        sort_all()
+
+    @pl.when(group == helper)
+    def _():
+        wait_rows(0)
+        receive(adj, rows_all, adj_sem, False, outgoing, False)
+        first_layer()
+        sort_all()
 
     @pl.when(group > 0)
     def _():
-        with jax.named_scope("sorta"):
-            for step, far in enumerate(near_first):
-                sort_share(far, step == 0, step == lines - 1)
-
-    with jax.named_scope("gram"):
-        quad = chunk // band
-        view = (MATES + 2) * band
-        gram = jnp.zeros((2 * band, view), F32)
-        for n in range(harm // chunk):
-            start = (MATES * clan + quad * n) * band
-            window = []
-            for k in range(quad):
-                buffer = shifted if k % 2 else lined
-                at = pl.ds(pl.multiple_of(start + (k - k % 2) * band, 2 * band), view)
-                window.append(buffer[:, at])
-            gram += jnp.dot(factor[n], jnp.concatenate(window, axis=0), preferred_element_type=F32)
-        for m in range(MATES):
-            if m % 2:
-                both = gram[:, (m - 1) * band : (m + 3) * band]
-                turned = pltpu.roll(both, 2 * band + 1, 1, stride=1, stride_axis=0)[:, : 2 * band]
-            else:
-                both = gram[:, m * band : (m + 2) * band]
-                turned = pltpu.roll(both, band + 1, 1, stride=1, stride_axis=0)
-            real = jnp.sum(turned[:band], axis=0, keepdims=True)
-            imag = jnp.sum(turned[band:], axis=0, keepdims=True)
-            partial[m] = jnp.where(lane < band, real, imag)
-
-    with jax.named_scope("reduce"):
+        correlate(factor, partial)
         to_mates(partial, gathered, 8, part_sem)
 
+    @pl.when(group == helper)
+    def _():
+        wait_rows(1)
+        with jax.named_scope("wait_factor"):
+            wait_for(factor_two, harm // chunk, hand_sem.at[1])
+        receive(adj_two, rows_two, two_sem, True, outgoing_two, True)
+        correlate(factor_two, partial_two)
+        to_sibling_mates(partial_two, gathered, 14, part_sem)
+
     with jax.named_scope("land"):
-        wait_for(landed, MATES - 1, land_sem)
+        @pl.when(chain)
+        def _():
+            wait_for(landed, MATES - 1, land_sem)
+
+        @pl.when(jnp.logical_not(chain))
+        def _():
+            wait_for(landed, MATES, land_sem)
+
         pieces = [landed[m].astype(F32) for m in range(MATES)]
         for plane in range(2):
             for upper in range(2):
@@ -490,7 +556,14 @@
                 bound_ref[0, plane, pl.ds(upper * half, half), :] = tile.astype(BF16)
 
     with jax.named_scope("sum"):
-        wait_for(gathered, MATES - 1, part_sem)
+        @pl.when(group > 0)
+        def _():
+            wait_for(gathered, MATES - 1, part_sem)
+
+        @pl.when(group == 0)
+        def _():
+            wait_for(gathered, MATES, part_sem)
+
         total = gathered[0]
         for m in range(1, MATES):
             total = total + gathered[m]
@@ -499,28 +572,41 @@
         grads_ref[0, 1:2, :] = total[:, band:]
 
     with jax.named_scope("drain"):
-        wait_for(rows_all, 2, send_sem.at[0])
-        wait_for(rows_all, 1, send_sem.at[1])
         wait_for(stage_fld, MATES - 1, send_sem.at[2])
         wait_for(fwd, peers - MATES, send_sem.at[3])
-        wait_for(landed, MATES - 1, send_sem.at[7])
-        wait_for(gathered, MATES - 1, send_sem.at[8])
+
+        @pl.when(chain)
+        def _():
+            for turn in (0, 1):
+                wait_for(rows_all, 2, send_sem.at[9 * turn])
+                wait_for(rows_all, 1, send_sem.at[9 * turn + 1])
+            wait_for(stage_src, MATES - 1, send_sem.at[4])
+            wait_for(adj, peers - MATES, send_sem.at[6])
+            wait_for(landed, MATES - 1, send_sem.at[7])
+            wait_for(landed, MATES, send_sem.at[13])
+
+        @pl.when(jnp.logical_not(chain))
+        def _():
+            wait_for(rows_all, 1, send_sem.at[11])
+
+        @pl.when(group > 0)
+        def _():
+            wait_for(gathered, MATES - 1, send_sem.at[8])
+
+        @pl.when(group == top)
+        def _():
+            wait_for(adj, MATES * len(near), send_sem.at[5])
+            wait_for(adj, peers, send_sem.at[12])
+            wait_for(adj, peers, send_sem.at[15])
 
         @pl.when(group == helper)
         def _():
             wait_for(adj, MATES * len(far), send_sem.at[5])
-
-        @pl.when((group == top) | (group == helper))
-        def _():
-            wait_for(stage_src, MATES - 1, send_sem.at[4])
-
-        @pl.when(group == top)
-        def _():
-            wait_for(adj, MATES * len(near), send_sem.at[5])
-
-        @pl.when(group > 0)
-        def _():
-            wait_for(adj, peers, send_sem.at[6])
+            wait_for(gathered, MATES, send_sem.at[14])
+
+        @pl.when(group == 0)
+        def _():
+            wait_for(factor, harm // chunk, send_sem.at[16])
 
 
 def solution(mesh):
@@ -546,24 +632,25 @@
                 pltpu.VMEM((2, rows, cols), BF16),
                 pltpu.VMEM((2, rows, cols), BF16),
                 pltpu.VMEM((1, harm), jnp.int32),
-                pltpu.VMEM((MATES, 2, rows, harm), BF16),
-                pltpu.VMEM((peers, *tile), BF16),
-                pltpu.VMEM((peers, *tile), BF16),
+                pltpu.VMEM((2, rows, harm), BF16),
+                *[pltpu.VMEM((MATES, 2, rows, harm), BF16)] * 2,
+                *[pltpu.VMEM((peers, *tile), BF16)] * 3,
                 pltpu.VMEM((harm, cols), BF16),
                 pltpu.VMEM((harm, cols), F32),
                 pltpu.VMEM((harm, harm), BF16),
                 pltpu.VMEM((harm, harm + 2 * cols), BF16),
                 pltpu.VMEM((2 * cols // MATES, 3 * harm), BF16),
                 pltpu.VMEM((2 * cols // MATES, 3 * harm), BF16),
-                pltpu.VMEM((harm // chunk, 2 * band, chunk // band * 2 * (cols // MATES)), BF16),
-                *[pltpu.VMEM((MATES, *tile), BF16)] * 6,
-                pltpu.VMEM((MATES, 1, cols), F32),
-                pltpu.VMEM((MATES, 1, cols), F32),
+                *[pltpu.VMEM((harm // chunk, 2 * band, chunk // band * 2 * (cols // MATES)), BF16)] * 2,
+                *[pltpu.VMEM((MATES, *tile), BF16)] * 7,
+                *[pltpu.VMEM((MATES, 1, cols), F32)] * 3,
                 pltpu.VMEM((2 * cols // MATES, harm + 2 * cols), F32),
                 pltpu.SemaphoreType.DMA((4,)),
-                pltpu.SemaphoreType.DMA((9,)),
-                pltpu.SemaphoreType.DMA((6,)),
+                pltpu.SemaphoreType.DMA((17,)),
+                pltpu.SemaphoreType.DMA((12,)),
                 pltpu.SemaphoreType.DMA((LINES,)),
+                pltpu.SemaphoreType.DMA((LINES,)),
+                pltpu.SemaphoreType.DMA((2,)),
                 pltpu.SemaphoreType.DMA,
                 pltpu.SemaphoreType.DMA((2,)),
                 pltpu.SemaphoreType.DMA,

time: 45.1 us -> 43.3 us (0.960)
  Pallas kernels: 43.1 us -> 41.2 us
    pallas_call x1, Pallas kernels: 43.1 us -> 41.2 us  [per_device(): pl.pallas_call(functools.partial(kernel, layers, peers, 1.0 / math.sqrt(h...]
where the time goes in v6:
time: 43.3 us; the launch traced here: 43 us
  Pallas kernels  41.2 us (95%)
  local copies, waits for them, and re-layouts  1.17 us (3%)
  between operations  0.64 us (1%)
    pallas_call x1, Pallas kernels, per_device(): pl.pallas_call(functools.partial(kernel, layers, peers, 1.0 / math.sqrt(h...  41.2 us
    unnamed x2, local copies, waits for them, and re-layouts  1.17 us

profile of v6, /device:TPU:2, one launch (start us, length us, event | category | flops | bytes accessed | tf_op | source)
XLA Modules:
  0.0 43.0 jit_solution(15196978603656795900)
XLA Ops:
  0.6 41.2 %shard_map.59 = (f32[1,2,64]{2,1,0:T(2,128)S(1)}, bf16[1,2,32,128]{3,2,1,0:T(8,128)(2,1)S(1)}) custom-call(bf16[2,32,128]{2,1,0:T(8,128)(2,1)} %source_hbm.1, bf16[1,2,32,2048]{3,2,1,0:T(8,128)(2,1)} %transfer_hbm.1, bf16[1,2,32,128]{3,2,1,0:T(8,128)(2,1)} %fields_hbm.1, s32[1,2048]{1,0:T(1,128)} %bitcast.1), custom_call_target="tpu_custom_call" | custom-call | tf_op jit(solution)/shard_map/pallas_call | solution.py:623
  41.8 0.6 %copy.8 = f32[1,2,64]{2,1,0:T(2,128)} copy(f32[1,2,64]{2,1,0:T(2,128)S(1)} %get-tuple-element.4) | data formatting | bytes 1024
  42.4 0.6 %copy.9 = bf16[1,2,32,128]{3,2,1,0:T(8,128)(2,1)} copy(bf16[1,2,32,128]{3,2,1,0:T(8,128)(2,1)S(1)} %get-tuple-element.5) | data formatting | bytes 32768

commit v7 on v6

--- a/solution.py
+++ b/solution.py
@@ -53,9 +53,6 @@
         pltpu.make_async_copy(fields_hbm.at[0], fields, load_sem.at[2]),
         pltpu.make_async_copy(orders_hbm, orders, load_sem.at[1]),
     ]
-    for load in loads:
-        load.start()
-
     barrier = pltpu.get_barrier_semaphore()
 
     def mate_index(j):
@@ -89,6 +86,9 @@
             pl.semaphore_signal(
                 barrier, inc=1, device_id=(helper, clan_index(far_line, 0)), device_id_type=MESH
             )
+
+    for load in loads:
+        load.start()
 
     lane = lax.broadcasted_iota(jnp.int32, (1, cols), 1)
     in_slice = lax.rem(lane, 2 * slice_b)
@@ -217,9 +217,9 @@
             def _():
                 pl.semaphore_signal(clear_sem, inc=1, device_id=(top, me), device_id_type=MESH)
 
-    def remote(src, dst, sem, arrived, target, index):
+    def remote(src, dst, arrived, target, index):
         return pltpu.make_async_remote_copy(
-            src_ref=src, dst_ref=dst, send_sem=send_sem.at[sem], recv_sem=arrived,
+            src_ref=src, dst_ref=dst, send_sem=send_sem, recv_sem=arrived,
             device_id=(target, index), device_id_type=MESH,
         )
 
@@ -227,19 +227,19 @@
         part_of = buffer.at[pl.ds(0, count)]
         pltpu.make_async_copy(part_of, part_of, sem).wait()
 
-    def to_mates(tiles, dst, sem, arrived):
+    def to_mates(tiles, dst, arrived):
         for j in (2, 1, 3):
             other = lax.rem(mate + j, MATES)
             remote(
-                tiles.at[other], dst.at[mate], sem, arrived, group, clan * MATES + other
+                tiles.at[other], dst.at[mate], arrived, group, clan * MATES + other
             ).start()
         dst[mate] = tiles[mate]
 
     clan_tiles = pl.ds(clan * MATES, MATES)
 
-    def to_clans(tiles, dst, sem, arrived, target, to):
+    def to_clans(tiles, dst, arrived, target, to):
         for a, b in to:
-            remote(tiles, dst.at[clan_tiles], sem, arrived, target, clan_index(a, b)).start()
+            remote(tiles, dst.at[clan_tiles], arrived, target, clan_index(a, b)).start()
 
     right, left = mate_index(1), mate_index(MATES - 1)
     from_left, from_right = lax.rem(mate + MATES - 1, MATES), lax.rem(mate + 1, MATES)
@@ -248,43 +248,42 @@
         for first in (0, 1):
             to_right = buffer.at[mate, first]
             to_left = buffer.at[mate, 1 - first]
-            for block, to, sem in ((to_right, right, 2 * first), (to_left, left, 2 * first + 1)):
-                remote(block, block, 9 * turn, rows_sem.at[6 * turn + sem], group, to).start()
+            for block, to, sem in ((to_right, right, 0), (to_left, left, 1)):
+                remote(block, block, rows_sem.at[3 * turn + (2 if first else sem)], group, to).start()
 
     def wait_half(turn, sem):
-        wait_for(rows_all.at[0], 1, rows_sem.at[6 * turn + sem])
+        wait_for(rows_all.at[0], 1, rows_sem.at[3 * turn + sem])
 
     def relay_rows(buffer, turn):
         with jax.named_scope("relay_t%d" % turn):
             wait_half(turn, 0)
             block = buffer.at[from_left, 0]
-            remote(block, block, 9 * turn + 1, rows_sem.at[6 * turn + 4], group, right).start()
+            remote(block, block, rows_sem.at[3 * turn + 2], group, right).start()
             wait_half(turn, 1)
             block = buffer.at[from_right, 1]
-            remote(block, block, 9 * turn + 1, rows_sem.at[6 * turn + 5], group, left).start()
+            remote(block, block, rows_sem.at[3 * turn + 2], group, left).start()
 
     def wait_rows(turn):
         with jax.named_scope("wait_t%d" % turn):
-            for k in (2, 3, 4, 5):
-                wait_half(turn, k)
-
-    def to_sibling(src, dst, sem, arrived):
-        remote(src, dst, sem, arrived, sibling, me).start()
-
-    def to_sibling_mates(tiles, dst, sem, arrived):
+            wait_for(rows_all, 2, rows_sem.at[3 * turn + 2])
+
+    def to_sibling(src, dst, arrived):
+        remote(src, dst, arrived, sibling, me).start()
+
+    def to_sibling_mates(tiles, dst, arrived):
         for j in (2, 1, 3, 0):
             other = lax.rem(mate + j, MATES)
             remote(
-                tiles.at[other], dst.at[mate], sem, arrived, sibling, clan * MATES + other
+                tiles.at[other], dst.at[mate], arrived, sibling, clan * MATES + other
             ).start()
 
     def start_fields():
-        to_mates(packed_fld, stage_fld, 2, stage_sem.at[0])
+        to_mates(packed_fld, stage_fld, stage_sem.at[0])
 
     def relay_fields():
         with jax.named_scope("relay_f"):
             wait_for(stage_fld, MATES - 1, stage_sem.at[0])
-            to_clans(stage_fld, fwd, 3, fwd_sem, group, offsets[:-1])
+            to_clans(stage_fld, fwd, fwd_sem, group, offsets[:-1])
             fwd[clan_tiles] = stage_fld[...]
 
     with jax.named_scope("spread"):
@@ -295,11 +294,11 @@
         def relay_source(to):
             with jax.named_scope("relay_s"):
                 wait_for(stage_src, MATES - 1, stage_sem.at[1])
-                to_clans(stage_src, adj, 5, adj_sem.at[line], top, to)
+                to_clans(stage_src, adj, adj_sem.at[line], top, to)
 
         @pl.when(group == top)
         def _():
-            to_mates(packed_src, stage_src, 4, stage_sem.at[1])
+            to_mates(packed_src, stage_src, stage_sem.at[1])
             start_rows(rows_all, 0)
             near_here()
             relay_source(near)
@@ -312,7 +311,7 @@
 
         @pl.when(group == helper)
         def _():
-            to_mates(packed_src, stage_src, 4, stage_sem.at[1])
+            to_mates(packed_src, stage_src, stage_sem.at[1])
             near_here()
             relay_source(far)
             all_here()
@@ -329,7 +328,7 @@
 
         @pl.when(jnp.logical_not(chain))
         def _():
-            to_sibling(rows_all.at[mate], rows_two.at[mate], 11, hand_sem.at[0])
+            to_sibling(rows_all.at[mate], rows_two.at[mate], hand_sem.at[0])
             near_here()
             all_here()
             start_fields()
@@ -385,42 +384,50 @@
             shifted[:, pl.ds(border - cols, cols)] = jnp.where(lane < cols // 2, 0.0, tail).astype(BF16)
 
     near_first = by_distance(lines)[::-1]
+    one_by_one = [[far] for far in near_first]
+    near_and_rest = [near_first[:1], near_first[1:]]
 
     def receive(tiles, block_rows, sems, own_there, out, sort):
         lower = jnp.zeros((MATES * 2 * rows, cols), F32)
         upper = jnp.zeros((MATES * 2 * rows, cols), F32)
-        for step, far in enumerate(near_first):
-            z = lax.rem(line + far, lines)
+        turns = one_by_one if sort else near_and_rest
+        for step, fars in enumerate(turns):
+            spots = [lax.rem(line + far, lines) for far in fars]
             with jax.named_scope("wait_a%d" % step):
-                wait_for(tiles, MATES * (planes - (own_there and step == 0)), sems.at[z])
+                for z in spots:
+                    wait_for(tiles, MATES * (planes - (own_there and step == 0)), sems.at[z])
             with jax.named_scope("propagate"):
-                packed = share_tiles(tiles, z)
-                at = pl.ds(pl.multiple_of(z * share, share), share // 2)
-                lower += jnp.dot(
-                    block_rows[:, :, :, at].reshape(MATES * 2 * rows, share // 2),
-                    packed, preferred_element_type=F32,
+                for z in spots:
+                    packed = share_tiles(tiles, z)
+                    at = pl.ds(pl.multiple_of(z * share, share), share // 2)
+                    lower += jnp.dot(
+                        block_rows[:, :, :, at].reshape(MATES * 2 * rows, share // 2),
+                        packed, preferred_element_type=F32,
+                    )
+                    at = pl.ds(pl.multiple_of(z * share + share // 2, share // 2), share // 2)
+                    upper += jnp.dot(
+                        block_rows[:, :, :, at].reshape(MATES * 2 * rows, share // 2),
+                        packed, preferred_element_type=F32,
+                    )
+            last = step == len(turns) - 1
+            if last:
+                mixed = jnp.where(lane < cols // 2, lower, upper).reshape(MATES, 2, rows, cols)
+                head, rest = mixed[:, :, :half], mixed[:, :, half:]
+                here = jnp.where(lane < cols // 2, head, rest)
+                there = jnp.where(lane < cols // 2, rest, head).reshape(MATES * 2 * half, cols)
+                total = here + pltpu.roll(there, cols // 2, 1).reshape(MATES, 2, half, cols)
+                cross = total[:, 1].reshape(MATES * half, cols)
+                cross = jnp.where(
+                    in_slice < slice_b,
+                    -pltpu.roll(cross, cols - slice_b, 1),
+                    pltpu.roll(cross, slice_b, 1),
                 )
-                at = pl.ds(pl.multiple_of(z * share + share // 2, share // 2), share // 2)
-                upper += jnp.dot(
-                    block_rows[:, :, :, at].reshape(MATES * 2 * rows, share // 2),
-                    packed, preferred_element_type=F32,
-                )
-            last = step == lines - 1
-            if last:
-                mixed = jnp.where(lane < cols // 2, lower, upper)
-                total = mixed + pltpu.roll(mixed, cols // 2, 1)
-                total = total.reshape(MATES, 2, rows, cols)
-                cross = pltpu.roll(total[:, 1].reshape(MATES * rows, cols), slice_b, 1)
-                cross = cross.reshape(MATES, rows, cols)
-                result = total[:, 0] + jnp.where(in_slice < slice_b, -cross, cross)
-                out[...] = jnp.where(
-                    lane < cols // 2, result[:, :half], result[:, half:]
-                ).astype(BF16)
+                out[...] = (total[:, 0] + cross.reshape(MATES, half, cols)).astype(BF16)
                 if sort:
-                    to_sibling_mates(out, landed, 13, land_sem)
+                    to_sibling_mates(out, landed, land_sem)
             if sort:
                 with jax.named_scope("sort0"):
-                    sort_share(tiles, far, step == 0, last)
+                    sort_share(tiles, fars[0], step == 0, last)
 
     def sort_all():
         with jax.named_scope("sorta"):
@@ -429,9 +436,9 @@
 
     def first_layer():
         with jax.named_scope("forward1"):
-            to_clans(outgoing, adj_two, 6, two_sem.at[line], group, offsets[:-1])
+            to_clans(outgoing, adj_two, two_sem.at[line], group, offsets[:-1])
             adj_two[clan_tiles] = outgoing[...]
-            to_mates(outgoing, landed, 7, land_sem)
+            to_mates(outgoing, landed, land_sem)
 
     @pl.when(group == top)
     def _():
@@ -445,9 +452,9 @@
         pl.semaphore_signal(go_sem, inc=1, device_id=(sibling, me), device_id_type=MESH)
         receive(adj_two, rows_two, two_sem, True, outgoing_two, False)
         with jax.named_scope("forward2"):
-            to_clans(outgoing_two, adj, 12, adj_sem.at[line], helper, offsets)
-            to_sibling(adj_two, adj, 15, hand_sem.at[1])
-            to_sibling_mates(outgoing_two, landed, 13, land_sem)
+            to_clans(outgoing_two, adj, adj_sem.at[line], helper, offsets)
+            to_sibling(adj_two, adj, hand_sem.at[1])
+            to_sibling_mates(outgoing_two, landed, land_sem)
         relay_fields()
         build_adj()
         sort_all()
@@ -506,7 +513,7 @@
 
     @pl.when(group == 0)
     def _():
-        to_sibling(factor, factor_two, 16, hand_sem.at[1])
+        to_sibling(factor, factor_two, hand_sem.at[1])
 
     @pl.when(group == top - 1)
     def _():
@@ -524,7 +531,7 @@
     @pl.when(group > 0)
     def _():
         correlate(factor, partial)
-        to_mates(partial, gathered, 8, part_sem)
+        to_mates(partial, gathered, part_sem)
 
     @pl.when(group == helper)
     def _():
@@ -533,7 +540,7 @@
             wait_for(factor_two, harm // chunk, hand_sem.at[1])
         receive(adj_two, rows_two, two_sem, True, outgoing_two, True)
         correlate(factor_two, partial_two)
-        to_sibling_mates(partial_two, gathered, 14, part_sem)
+        to_sibling_mates(partial_two, gathered, part_sem)
 
     with jax.named_scope("land"):
         @pl.when(chain)
@@ -572,41 +579,52 @@
         grads_ref[0, 1:2, :] = total[:, band:]
 
     with jax.named_scope("drain"):
-        wait_for(stage_fld, MATES - 1, send_sem.at[2])
-        wait_for(fwd, peers - MATES, send_sem.at[3])
+        wait_for(stage_fld, MATES - 1, send_sem)
+        wait_for(fwd, peers - MATES, send_sem)
 
         @pl.when(chain)
         def _():
             for turn in (0, 1):
-                wait_for(rows_all, 2, send_sem.at[9 * turn])
-                wait_for(rows_all, 1, send_sem.at[9 * turn + 1])
-            wait_for(stage_src, MATES - 1, send_sem.at[4])
-            wait_for(adj, peers - MATES, send_sem.at[6])
-            wait_for(landed, MATES - 1, send_sem.at[7])
-            wait_for(landed, MATES, send_sem.at[13])
+                wait_for(rows_all, 2, send_sem)
+                wait_for(rows_all, 1, send_sem)
+            wait_for(stage_src, MATES - 1, send_sem)
+            wait_for(adj, peers - MATES, send_sem)
+            wait_for(landed, MATES - 1, send_sem)
+            wait_for(landed, MATES, send_sem)
 
         @pl.when(jnp.logical_not(chain))
         def _():
-            wait_for(rows_all, 1, send_sem.at[11])
+            wait_for(rows_all, 1, send_sem)
 
         @pl.when(group > 0)
         def _():
-            wait_for(gathered, MATES - 1, send_sem.at[8])
+            wait_for(gathered, MATES - 1, send_sem)
 
         @pl.when(group == top)
         def _():
-            wait_for(adj, MATES * len(near), send_sem.at[5])
-            wait_for(adj, peers, send_sem.at[12])
-            wait_for(adj, peers, send_sem.at[15])
+            wait_for(adj, MATES * len(near), send_sem)
+            wait_for(adj, peers, send_sem)
+            wait_for(adj, peers, send_sem)
 
         @pl.when(group == helper)
         def _():
-            wait_for(adj, MATES * len(far), send_sem.at[5])
-            wait_for(gathered, MATES, send_sem.at[14])
+            wait_for(adj, MATES * len(far), send_sem)
+            wait_for(gathered, MATES, send_sem)
 
         @pl.when(group == 0)
         def _():
-            wait_for(factor, harm // chunk, send_sem.at[16])
+            wait_for(factor, harm // chunk, send_sem)
+
+
+def put_out(grads_ref, bound_ref, grads_hbm, bound_hbm, sems):
+    copies = [
+        pltpu.make_async_copy(bound_ref, bound_hbm, sems.at[0]),
+        pltpu.make_async_copy(grads_ref, grads_hbm, sems.at[1]),
+    ]
+    for copy in copies:
+        copy.start()
+    for copy in copies:
+        copy.wait()
 
 
 def solution(mesh):
@@ -620,7 +638,7 @@
         vmem = pl.BlockSpec(memory_space=pltpu.VMEM)
         hbm = pl.BlockSpec(memory_space=pltpu.HBM)
         tile = (rows // 2, cols)
-        return pl.pallas_call(
+        made = pl.pallas_call(
             functools.partial(kernel, layers, peers, 1.0 / math.sqrt(harm * cols)),
             out_shape=(
                 jax.ShapeDtypeStruct((1, 2, band), F32),
@@ -646,8 +664,8 @@
                 *[pltpu.VMEM((MATES, 1, cols), F32)] * 3,
                 pltpu.VMEM((2 * cols // MATES, harm + 2 * cols), F32),
                 pltpu.SemaphoreType.DMA((4,)),
-                pltpu.SemaphoreType.DMA((17,)),
-                pltpu.SemaphoreType.DMA((12,)),
+                pltpu.SemaphoreType.DMA,
+                pltpu.SemaphoreType.DMA((6,)),
                 pltpu.SemaphoreType.DMA((LINES,)),
                 pltpu.SemaphoreType.DMA((LINES,)),
                 pltpu.SemaphoreType.DMA((2,)),
@@ -666,6 +684,14 @@
                 for value in (source, transfer, fields, orders.reshape(1, harm))
             )
         )
+        return pl.pallas_call(
+            put_out,
+            out_shape=[jax.ShapeDtypeStruct(value.shape, value.dtype) for value in made],
+            in_specs=[vmem] * 2,
+            out_specs=[hbm] * 2,
+            scratch_shapes=[pltpu.SemaphoreType.DMA((2,))],
+            compiler_params=pltpu.CompilerParams(vmem_limit_bytes=1 << 20),
+        )(*(pltpu.with_memory_space_constraint(value, pltpu.VMEM) for value in made))
 
     return jax.shard_map(
         per_device,

time: 43.3 us -> 42.5 us (0.982)
  local copies, waits for them, and re-layouts: 1.17 us -> 0 us
  Pallas kernels: 41.2 us -> 41.8 us
    unnamed x2 -> x0, local copies, waits for them, and re-layouts: 1.17 us -> none
    pallas_call x0 -> x1, Pallas kernels: none -> 0.63 us  [per_device(): pl.pallas_call(put_out, out_shape=[jax.ShapeDtypeStruct(value.shape, valu...]
where the time goes in v7:
time: 42.5 us; the launch traced here: 42.4 us
  Pallas kernels  41.8 us (98%)
  between operations  0.64 us (2%)
    pallas_call x1, Pallas kernels, per_device(): pl.pallas_call(functools.partial(kernel, layers, peers, 1.0 / math.sqrt(h...  41.2 us

profile of v7, /device:TPU:2, one launch (start us, length us, event | category | flops | bytes accessed | tf_op | source)
XLA Modules:
  0.0 42.4 jit_solution(5817955725491009530)
XLA Ops:
  0.6 41.2 %shard_map.59 = (f32[1,2,64]{2,1,0:T(2,128)S(1)}, bf16[1,2,32,128]{3,2,1,0:T(8,128)(2,1)S(1)}) custom-call(bf16[2,32,128]{2,1,0:T(8,128)(2,1)} %source_hbm.1, bf16[1,2,32,2048]{3,2,1,0:T(8,128)(2,1)} %transfer_hbm.1, bf16[1,2,32,128]{3,2,1,0:T(8,128)(2,1)} %fields_hbm.1, s32[1,2048]{1,0:T(1,128)} %bitcast.1), custom_call_target="tpu_custom_call" | custom-call | tf_op jit(solution)/shard_map/pallas_call | solution.py:641
  41.8 0.6 %shard_map.60 = (f32[1,2,64]{2,1,0:T(2,128)}, bf16[1,2,32,128]{3,2,1,0:T(8,128)(2,1)}) custom-call(f32[1,2,64]{2,1,0:T(2,128)S(1)} %get-tuple-element.4.grads_ref, bf16[1,2,32,128]{3,2,1,0:T(8,128)(2,1)S(1)} %get-tuple-element.5.bound_ref), custom_call_target="tpu_custom_call" | custom-call | tf_op jit(solution)/shard_map/pallas_call | solution.py:687

commit v8 on v7

--- a/solution.py
+++ b/solution.py
@@ -320,25 +320,35 @@
             build_fwd()
             relay_fields()
             relay_rows(rows_all, 0)
-            wait_for(rows_all, 1, hand_sem.at[0])
-            start_rows(rows_two, 1)
             build_adj()
-            relay_rows(rows_two, 1)
             pl.semaphore_wait(clear_sem, 1)
+            pl.semaphore_signal(go_sem, inc=1, device_id=(sibling, me), device_id_type=MESH)
 
         @pl.when(jnp.logical_not(chain))
         def _():
-            to_sibling(rows_all.at[mate], rows_two.at[mate], hand_sem.at[0])
+            @pl.when(group == top - 1)
+            def _():
+                to_sibling(rows_all.at[mate], rows_two.at[mate], hand_sem.at[0])
+
             near_here()
             all_here()
             start_fields()
+
+            @pl.when(group == 0)
+            def _():
+                start_rows(rows_all, 0)
+
             build_fwd()
 
             @pl.when(group == top - 1)
             def _():
                 build_adj()
-                pl.semaphore_wait(go_sem, 1)
-
+
+            @pl.when(group == 0)
+            def _():
+                relay_rows(rows_all, 0)
+
+            pl.semaphore_wait(go_sem, 1)
             relay_fields()
 
     def unpack(tiles):
@@ -355,18 +365,20 @@
             axis=0,
         )
 
-    def sort_share(tiles, far, first, last):
-        z = lax.rem(line + far, lines)
-        turned = share_tiles(tiles, z).astype(F32).T.astype(BF16)
-        left = jnp.concatenate([turned[: cols // 2], turned[cols // 2 :]], axis=1)
-        at = pl.ds(pl.multiple_of(z * share, share), share)
+    def sort_shares(tiles, fars, first, last):
+        shares = []
+        for far in fars:
+            z = lax.rem(line + far, lines)
+            turned = share_tiles(tiles, z).astype(F32).T.astype(BF16)
+            left = jnp.concatenate([turned[: cols // 2], turned[cols // 2 :]], axis=1)
+            shares.append((left, pl.ds(pl.multiple_of(z * share, share), share)))
         span = 3 * depth if wide % (3 * depth) == 0 else wide
         tail = None
         for k in reversed(range(wide // span)):
             here = pl.ds(k * span, span)
-            total = jnp.dot(left, hot_adj[at, here], preferred_element_type=F32)
-            if not first:
-                total += sorting[:, here]
+            total = jnp.zeros((cols // 2, span), F32) if first else sorting[:, here]
+            for left, at in shares:
+                total += jnp.dot(left, hot_adj[at, here], preferred_element_type=F32)
             if not last:
                 sorting[:, here] = total
                 continue
@@ -384,14 +396,12 @@
             shifted[:, pl.ds(border - cols, cols)] = jnp.where(lane < cols // 2, 0.0, tail).astype(BF16)
 
     near_first = by_distance(lines)[::-1]
-    one_by_one = [[far] for far in near_first]
     near_and_rest = [near_first[:1], near_first[1:]]
 
-    def receive(tiles, block_rows, sems, own_there, out, sort):
+    def receive(tiles, block_rows, sems, own_there, out):
         lower = jnp.zeros((MATES * 2 * rows, cols), F32)
         upper = jnp.zeros((MATES * 2 * rows, cols), F32)
-        turns = one_by_one if sort else near_and_rest
-        for step, fars in enumerate(turns):
+        for step, fars in enumerate(near_and_rest):
             spots = [lax.rem(line + far, lines) for far in fars]
             with jax.named_scope("wait_a%d" % step):
                 for z in spots:
@@ -409,8 +419,7 @@
                         block_rows[:, :, :, at].reshape(MATES * 2 * rows, share // 2),
                         packed, preferred_element_type=F32,
                     )
-            last = step == len(turns) - 1
-            if last:
+            if step == len(near_and_rest) - 1:
                 mixed = jnp.where(lane < cols // 2, lower, upper).reshape(MATES, 2, rows, cols)
                 head, rest = mixed[:, :, :half], mixed[:, :, half:]
                 here = jnp.where(lane < cols // 2, head, rest)
@@ -423,16 +432,22 @@
                     pltpu.roll(cross, slice_b, 1),
                 )
                 out[...] = (total[:, 0] + cross.reshape(MATES, half, cols)).astype(BF16)
-                if sort:
-                    to_sibling_mates(out, landed, land_sem)
-            if sort:
-                with jax.named_scope("sort0"):
-                    sort_share(tiles, fars[0], step == 0, last)
+
+    def receive_sorted(tiles, sems):
+        for step, fars in enumerate(near_and_rest):
+            for far in fars:
+                z = lax.rem(line + far, lines)
+                with jax.named_scope("wait_s%d" % far):
+                    wait_for(tiles, MATES * (planes - (step == 0)), sems.at[z])
+                for p in range(planes):
+                    block = pl.ds((p * lines + z) * MATES, MATES)
+                    to_sibling(tiles.at[block], tiles.at[block], sems.at[z])
+            with jax.named_scope("sort0"):
+                sort_shares(tiles, fars, step == 0, step == len(near_and_rest) - 1)
 
     def sort_all():
         with jax.named_scope("sorta"):
-            for step, far in enumerate(near_first):
-                sort_share(adj, far, step == 0, step == lines - 1)
+            sort_shares(adj, near_first, True, True)
 
     def first_layer():
         with jax.named_scope("forward1"):
@@ -443,14 +458,14 @@
     @pl.when(group == top)
     def _():
         wait_rows(0)
-        receive(adj, rows_all, adj_sem, True, outgoing, False)
+        receive(adj, rows_all, adj_sem, True, outgoing)
         first_layer()
         relay_rows(rows_two, 1)
         start_fields()
         build_fwd()
         wait_rows(1)
         pl.semaphore_signal(go_sem, inc=1, device_id=(sibling, me), device_id_type=MESH)
-        receive(adj_two, rows_two, two_sem, True, outgoing_two, False)
+        receive(adj_two, rows_two, two_sem, True, outgoing_two)
         with jax.named_scope("forward2"):
             to_clans(outgoing_two, adj, adj_sem.at[line], helper, offsets)
             to_sibling(adj_two, adj, hand_sem.at[1])
@@ -514,6 +529,9 @@
     @pl.when(group == 0)
     def _():
         to_sibling(factor, factor_two, hand_sem.at[1])
+        wait_rows(0)
+        receive(adj_two, rows_all, two_sem, False, outgoing)
+        to_mates(outgoing, landed, land_sem)
 
     @pl.when(group == top - 1)
     def _():
@@ -524,7 +542,7 @@
     @pl.when(group == helper)
     def _():
         wait_rows(0)
-        receive(adj, rows_all, adj_sem, False, outgoing, False)
+        receive(adj, rows_all, adj_sem, False, outgoing)
         first_layer()
         sort_all()
 
@@ -535,19 +553,18 @@
 
     @pl.when(group == helper)
     def _():
-        wait_rows(1)
         with jax.named_scope("wait_factor"):
             wait_for(factor_two, harm // chunk, hand_sem.at[1])
-        receive(adj_two, rows_two, two_sem, True, outgoing_two, True)
+        receive_sorted(adj_two, two_sem)
         correlate(factor_two, partial_two)
         to_sibling_mates(partial_two, gathered, part_sem)
 
     with jax.named_scope("land"):
-        @pl.when(chain)
+        @pl.when(group != top - 1)
         def _():
             wait_for(landed, MATES - 1, land_sem)
 
-        @pl.when(jnp.logical_not(chain))
+        @pl.when(group == top - 1)
         def _():
             wait_for(landed, MATES, land_sem)
 
@@ -582,29 +599,31 @@
         wait_for(stage_fld, MATES - 1, send_sem)
         wait_for(fwd, peers - MATES, send_sem)
 
+        @pl.when(group != top - 1)
+        def _():
+            wait_for(rows_all, 3, send_sem)
+            wait_for(landed, MATES - 1, send_sem)
+
         @pl.when(chain)
         def _():
-            for turn in (0, 1):
-                wait_for(rows_all, 2, send_sem)
-                wait_for(rows_all, 1, send_sem)
             wait_for(stage_src, MATES - 1, send_sem)
             wait_for(adj, peers - MATES, send_sem)
-            wait_for(landed, MATES - 1, send_sem)
+            wait_for(adj, peers, send_sem)
+
+        @pl.when(group > 0)
+        def _():
+            wait_for(gathered, MATES - 1, send_sem)
+
+        @pl.when(group == top)
+        def _():
+            wait_for(rows_all, 3, send_sem)
             wait_for(landed, MATES, send_sem)
-
-        @pl.when(jnp.logical_not(chain))
-        def _():
-            wait_for(rows_all, 1, send_sem)
-
-        @pl.when(group > 0)
-        def _():
-            wait_for(gathered, MATES - 1, send_sem)
-
-        @pl.when(group == top)
-        def _():
             wait_for(adj, MATES * len(near), send_sem)
             wait_for(adj, peers, send_sem)
-            wait_for(adj, peers, send_sem)
+
+        @pl.when(group == top - 1)
+        def _():
+            wait_for(rows_all, 1, send_sem)
 
         @pl.when(group == helper)
         def _():

time: 42.5 us -> 41.8 us (0.984)
  Pallas kernels: 41.8 us -> 40.9 us
    pallas_call x1, Pallas kernels: 41.2 us -> 40.3 us  [per_device(): pl.pallas_call(functools.partial(kernel, layers, peers, 1.0 / math.sqrt(h...]
where the time goes in v8:
time: 41.8 us; the launch traced here: 41.6 us
  Pallas kernels  40.9 us (98%)
  between operations  0.64 us (2%)
    pallas_call x1, Pallas kernels, per_device(): pl.pallas_call(functools.partial(kernel, layers, peers, 1.0 / math.sqrt(h...  40.3 us

profile of v8, /device:TPU:2, one launch (start us, length us, event | category | flops | bytes accessed | tf_op | source)
XLA Modules:
  0.0 41.6 jit_solution(7409764321978866219)
XLA Ops:
  0.6 40.3 %shard_map.59 = (f32[1,2,64]{2,1,0:T(2,128)S(1)}, bf16[1,2,32,128]{3,2,1,0:T(8,128)(2,1)S(1)}) custom-call(bf16[2,32,128]{2,1,0:T(8,128)(2,1)} %source_hbm.1, bf16[1,2,32,2048]{3,2,1,0:T(8,128)(2,1)} %transfer_hbm.1, bf16[1,2,32,128]{3,2,1,0:T(8,128)(2,1)} %fields_hbm.1, s32[1,2048]{1,0:T(1,128)} %bitcast.1), custom_call_target="tpu_custom_call" | custom-call | tf_op jit(solution)/shard_map/pallas_call | solution.py:660
  40.9 0.6 %shard_map.60 = (f32[1,2,64]{2,1,0:T(2,128)}, bf16[1,2,32,128]{3,2,1,0:T(8,128)(2,1)}) custom-call(f32[1,2,64]{2,1,0:T(2,128)S(1)} %get-tuple-element.4.grads_ref, bf16[1,2,32,128]{3,2,1,0:T(8,128)(2,1)S(1)} %get-tuple-element.5.bound_ref), custom_call_target="tpu_custom_call" | custom-call | tf_op jit(solution)/shard_map/pallas_call | solution.py:706

commit v9 on v8

--- a/solution.py
+++ b/solution.py
@@ -372,13 +372,15 @@
             turned = share_tiles(tiles, z).astype(F32).T.astype(BF16)
             left = jnp.concatenate([turned[: cols // 2], turned[cols // 2 :]], axis=1)
             shares.append((left, pl.ds(pl.multiple_of(z * share, share), share)))
+        left = jnp.concatenate([piece for piece, _ in shares], axis=1)
         span = 3 * depth if wide % (3 * depth) == 0 else wide
         tail = None
         for k in reversed(range(wide // span)):
             here = pl.ds(k * span, span)
-            total = jnp.zeros((cols // 2, span), F32) if first else sorting[:, here]
-            for left, at in shares:
-                total += jnp.dot(left, hot_adj[at, here], preferred_element_type=F32)
+            hot = jnp.concatenate([hot_adj[at, here] for _, at in shares], axis=0)
+            total = jnp.dot(left, hot, preferred_element_type=F32)
+            if not first:
+                total += sorting[:, here]
             if not last:
                 sorting[:, here] = total
                 continue
@@ -396,30 +398,35 @@
             shifted[:, pl.ds(border - cols, cols)] = jnp.where(lane < cols // 2, 0.0, tail).astype(BF16)
 
     near_first = by_distance(lines)[::-1]
-    near_and_rest = [near_first[:1], near_first[1:]]
+    by_arrival = [near_first[:1], near_first[1:-1], near_first[-1:]]
 
     def receive(tiles, block_rows, sems, own_there, out):
         lower = jnp.zeros((MATES * 2 * rows, cols), F32)
         upper = jnp.zeros((MATES * 2 * rows, cols), F32)
-        for step, fars in enumerate(near_and_rest):
+        for step, fars in enumerate(by_arrival):
             spots = [lax.rem(line + far, lines) for far in fars]
             with jax.named_scope("wait_a%d" % step):
                 for z in spots:
                     wait_for(tiles, MATES * (planes - (own_there and step == 0)), sems.at[z])
             with jax.named_scope("propagate"):
-                for z in spots:
-                    packed = share_tiles(tiles, z)
-                    at = pl.ds(pl.multiple_of(z * share, share), share // 2)
-                    lower += jnp.dot(
-                        block_rows[:, :, :, at].reshape(MATES * 2 * rows, share // 2),
-                        packed, preferred_element_type=F32,
+                packed = jnp.concatenate([share_tiles(tiles, z) for z in spots], axis=0)
+
+                def product(upper_half):
+                    starts = [z * share + upper_half * (share // 2) for z in spots]
+                    matrix = jnp.concatenate(
+                        [
+                            block_rows[
+                                :, :, :, pl.ds(pl.multiple_of(start, share // 2), share // 2)
+                            ].reshape(MATES * 2 * rows, share // 2)
+                            for start in starts
+                        ],
+                        axis=1,
                     )
-                    at = pl.ds(pl.multiple_of(z * share + share // 2, share // 2), share // 2)
-                    upper += jnp.dot(
-                        block_rows[:, :, :, at].reshape(MATES * 2 * rows, share // 2),
-                        packed, preferred_element_type=F32,
-                    )
-            if step == len(near_and_rest) - 1:
+                    return jnp.dot(matrix, packed, preferred_element_type=F32)
+
+                lower += product(0)
+                upper += product(1)
+            if step == len(by_arrival) - 1:
                 mixed = jnp.where(lane < cols // 2, lower, upper).reshape(MATES, 2, rows, cols)
                 head, rest = mixed[:, :, :half], mixed[:, :, half:]
                 here = jnp.where(lane < cols // 2, head, rest)
@@ -434,7 +441,8 @@
                 out[...] = (total[:, 0] + cross.reshape(MATES, half, cols)).astype(BF16)
 
     def receive_sorted(tiles, sems):
-        for step, fars in enumerate(near_and_rest):
+        sorts = [near_first[:1], near_first[1:2], near_first[2:]]
+        for step, fars in enumerate(by_arrival):
             for far in fars:
                 z = lax.rem(line + far, lines)
                 with jax.named_scope("wait_s%d" % far):
@@ -443,7 +451,7 @@
                     block = pl.ds((p * lines + z) * MATES, MATES)
                     to_sibling(tiles.at[block], tiles.at[block], sems.at[z])
             with jax.named_scope("sort0"):
-                sort_shares(tiles, fars, step == 0, step == len(near_and_rest) - 1)
+                sort_shares(tiles, sorts[step], step == 0, step == len(by_arrival) - 1)
 
     def sort_all():
         with jax.named_scope("sorta"):
@@ -487,12 +495,7 @@
         @pl.loop(0, harm // chunk)
         def _(r):
             at = pl.ds(pl.multiple_of(r * chunk, chunk), chunk)
-            total = jnp.zeros((chunk, cols), F32)
-            for k in range(steps):
-                total += jnp.dot(
-                    hot_fwd[at, pl.ds(k * depth, depth)], stretched[pl.ds(k * depth, depth), :],
-                    preferred_element_type=F32,
-                )
+            total = jnp.dot(hot_fwd[at, :], stretched[...], preferred_element_type=F32)
             real = total * sign
             imag = pltpu.roll(total, slice_b, 1)
             for pair in range(quads // 2):
@@ -506,15 +509,15 @@
         with jax.named_scope("gram"):
             quad = chunk // band
             view = (MATES + 2) * band
-            gram = jnp.zeros((2 * band, view), F32)
+            window = []
             for n in range(harm // chunk):
                 start = (MATES * clan + quad * n) * band
-                window = []
                 for k in range(quad):
                     buffer = shifted if k % 2 else lined
                     at = pl.ds(pl.multiple_of(start + (k - k % 2) * band, 2 * band), view)
                     window.append(buffer[:, at])
-                gram += jnp.dot(made[n], jnp.concatenate(window, axis=0), preferred_element_type=F32)
+            left = jnp.concatenate([made[n] for n in range(harm // chunk)], axis=1)
+            gram = jnp.dot(left, jnp.concatenate(window, axis=0), preferred_element_type=F32)
             for m in range(MATES):
                 if m % 2:
                     both = gram[:, (m - 1) * band : (m + 3) * band]

time: 41.8 us -> 41.6 us (level)
  no operation moved by 1% of the time
where the time goes in v9:
time: 41.6 us; the launch traced here: 41.5 us
  Pallas kernels  40.9 us (98%)
  between operations  0.64 us (2%)
    pallas_call x1, Pallas kernels, per_device(): pl.pallas_call(functools.partial(kernel, layers, peers, 1.0 / math.sqrt(h...  40.3 us

profile of v9, /device:TPU:2, one launch (start us, length us, event | category | flops | bytes accessed | tf_op | source)
XLA Modules:
  0.0 41.5 jit_solution(3886927812579757142)
XLA Ops:
  0.6 40.3 %shard_map.59 = (f32[1,2,64]{2,1,0:T(2,128)S(1)}, bf16[1,2,32,128]{3,2,1,0:T(8,128)(2,1)S(1)}) custom-call(bf16[2,32,128]{2,1,0:T(8,128)(2,1)} %source_hbm.1, bf16[1,2,32,2048]{3,2,1,0:T(8,128)(2,1)} %transfer_hbm.1, bf16[1,2,32,128]{3,2,1,0:T(8,128)(2,1)} %fields_hbm.1, s32[1,2048]{1,0:T(1,128)} %bitcast.1), custom_call_target="tpu_custom_call" | custom-call | tf_op jit(solution)/shard_map/pallas_call | solution.py:663
  40.9 0.6 %shard_map.60 = (f32[1,2,64]{2,1,0:T(2,128)}, bf16[1,2,32,128]{3,2,1,0:T(8,128)(2,1)}) custom-call(f32[1,2,64]{2,1,0:T(2,128)S(1)} %get-tuple-element.4.grads_ref, bf16[1,2,32,128]{3,2,1,0:T(8,128)(2,1)S(1)} %get-tuple-element.5.bound_ref), custom_call_target="tpu_custom_call" | custom-call | tf_op jit(solution)/shard_map/pallas_call | solution.py:709

commit v10 on v9

--- a/solution.py
+++ b/solution.py
@@ -471,6 +471,7 @@
         relay_rows(rows_two, 1)
         start_fields()
         build_fwd()
+        build_adj()
         wait_rows(1)
         pl.semaphore_signal(go_sem, inc=1, device_id=(sibling, me), device_id_type=MESH)
         receive(adj_two, rows_two, two_sem, True, outgoing_two)
@@ -478,9 +479,8 @@
             to_clans(outgoing_two, adj, adj_sem.at[line], helper, offsets)
             to_sibling(adj_two, adj, hand_sem.at[1])
             to_sibling_mates(outgoing_two, landed, land_sem)
+        sort_all()
         relay_fields()
-        build_adj()
-        sort_all()
 
     with jax.named_scope("wait_f"):
         wait_for(fwd, peers - MATES, fwd_sem)

time: 41.6 us -> 42.3 us (1.017)
  Pallas kernels: 40.9 us -> 41.4 us
    pallas_call x1, Pallas kernels: 40.3 us -> 40.8 us  [per_device(): pl.pallas_call(functools.partial(kernel, layers, peers, 1.0 / math.sqrt(h...]
where the time goes in v10:
time: 42.3 us; the launch traced here: 42 us
  Pallas kernels  41.4 us (98%)
  between operations  0.64 us (2%)
    pallas_call x1, Pallas kernels, per_device(): pl.pallas_call(functools.partial(kernel, layers, peers, 1.0 / math.sqrt(h...  40.8 us

profile of v10, /device:TPU:2, one launch (start us, length us, event | category | flops | bytes accessed | tf_op | source)
XLA Modules:
  0.0 42.0 jit_solution(11238945215198052879)
XLA Ops:
  0.6 40.8 %shard_map.59 = (f32[1,2,64]{2,1,0:T(2,128)S(1)}, bf16[1,2,32,128]{3,2,1,0:T(8,128)(2,1)S(1)}) custom-call(bf16[2,32,128]{2,1,0:T(8,128)(2,1)} %source_hbm.1, bf16[1,2,32,2048]{3,2,1,0:T(8,128)(2,1)} %transfer_hbm.1, bf16[1,2,32,128]{3,2,1,0:T(8,128)(2,1)} %fields_hbm.1, s32[1,2048]{1,0:T(1,128)} %bitcast.1), custom_call_target="tpu_custom_call" | custom-call | tf_op jit(solution)/shard_map/pallas_call | solution.py:663
  41.4 0.6 %shard_map.60 = (f32[1,2,64]{2,1,0:T(2,128)}, bf16[1,2,32,128]{3,2,1,0:T(8,128)(2,1)}) custom-call(f32[1,2,64]{2,1,0:T(2,128)S(1)} %get-tuple-element.4.grads_ref, bf16[1,2,32,128]{3,2,1,0:T(8,128)(2,1)S(1)} %get-tuple-element.5.bound_ref), custom_call_target="tpu_custom_call" | custom-call | tf_op jit(solution)/shard_map/pallas_call | solution.py:709

commit v11 on v9

--- a/solution.py
+++ b/solution.py
@@ -322,7 +322,6 @@
             relay_rows(rows_all, 0)
             build_adj()
             pl.semaphore_wait(clear_sem, 1)
-            pl.semaphore_signal(go_sem, inc=1, device_id=(sibling, me), device_id_type=MESH)
 
         @pl.when(jnp.logical_not(chain))
         def _():
@@ -484,6 +483,11 @@
 
     with jax.named_scope("wait_f"):
         wait_for(fwd, peers - MATES, fwd_sem)
+
+        @pl.when(group == helper)
+        def _():
+            pl.semaphore_signal(go_sem, inc=1, device_id=(sibling, me), device_id_type=MESH)
+
     with jax.named_scope("sortf"):
         for k in range(steps):
             count = depth // rows
@@ -556,9 +560,9 @@
 
     @pl.when(group == helper)
     def _():
+        receive_sorted(adj_two, two_sem)
         with jax.named_scope("wait_factor"):
             wait_for(factor_two, harm // chunk, hand_sem.at[1])
-        receive_sorted(adj_two, two_sem)
         correlate(factor_two, partial_two)
         to_sibling_mates(partial_two, gathered, part_sem)
 

time: 41.6 us -> 41.7 us (level)
  no operation moved by 1% of the time
where the time goes in v11:
time: 41.7 us; the launch traced here: 41.6 us
  Pallas kernels  40.9 us (98%)
  between operations  0.64 us (2%)
    pallas_call x1, Pallas kernels, per_device(): pl.pallas_call(functools.partial(kernel, layers, peers, 1.0 / math.sqrt(h...  40.3 us

profile of v11, /device:TPU:2, one launch (start us, length us, event | category | flops | bytes accessed | tf_op | source)
XLA Modules:
  0.0 41.6 jit_solution(4769510797040272274)
XLA Ops:
  0.6 40.3 %shard_map.59 = (f32[1,2,64]{2,1,0:T(2,128)S(1)}, bf16[1,2,32,128]{3,2,1,0:T(8,128)(2,1)S(1)}) custom-call(bf16[2,32,128]{2,1,0:T(8,128)(2,1)} %source_hbm.1, bf16[1,2,32,2048]{3,2,1,0:T(8,128)(2,1)} %transfer_hbm.1, bf16[1,2,32,128]{3,2,1,0:T(8,128)(2,1)} %fields_hbm.1, s32[1,2048]{1,0:T(1,128)} %bitcast.1), custom_call_target="tpu_custom_call" | custom-call | tf_op jit(solution)/shard_map/pallas_call | solution.py:667
  40.9 0.6 %shard_map.60 = (f32[1,2,64]{2,1,0:T(2,128)}, bf16[1,2,32,128]{3,2,1,0:T(8,128)(2,1)}) custom-call(f32[1,2,64]{2,1,0:T(2,128)S(1)} %get-tuple-element.4.grads_ref, bf16[1,2,32,128]{3,2,1,0:T(8,128)(2,1)S(1)} %get-tuple-element.5.bound_ref), custom_call_target="tpu_custom_call" | custom-call | tf_op jit(solution)/shard_map/pallas_call | solution.py:713
